TPU v7x, 16 devices: a 4x2x1 block of a 4x4x8 slice. The times are simulated.
16 devices in a mesh: dp: 4 (over y, z, core), tp: 4 (over x).
Axes of the slice: x: 4, y: 2, z: 1, core: 2. Of those that a mesh axis runs over, the one named last changes fastest.
The devices are a block of a 4x4x8 slice.
Arguments:
- x: bfloat16 [5632, 3072], P(('dp', 'tp')), parts along dimension 0
- dy: bfloat16 [5632, 3072], P(('dp', 'tp')), parts along dimension 0
- pre: bfloat16 [5632, 9216], P('dp', 'tp'), parts along dimension 0
- w_in: bfloat16 [3072, 9216], P(None, 'tp')
- w_down: bfloat16 [9216, 3072], P('tp')
Outputs:
- output 1: bfloat16 [5632, 3072], P(('dp', 'tp')), parts along dimension 0
- output 2: bfloat16 [12288, 9216], P('dp', 'tp'), parts along dimension 0
- output 3: bfloat16 [36864, 3072], P(('dp', 'tp')), parts along dimension 0
There are 4 independent parts. A program takes and returns all parts, laid end to end along the dimension named above; an argument that names none is the same for every part.
All inputs are finite; a program needn't handle non-finite values.
Results may differ from a plain program's by a relative error of at most 0.012.
Values are sent between devices in bfloat16 or wider.
A program may use at most 768 MiB of HBM per device.

v0:
```python
import functools

import jax
import jax.numpy as jnp
from jax import lax
from jax.experimental import pallas as pl
from jax.experimental.pallas import tpu as pltpu
from jax.sharding import PartitionSpec as P

NT = (((1,), (1,)), ((), ()))
TN = (((0,), (0,)), ((), ()))
F32, BF16 = jnp.float32, jnp.bfloat16
TILE = 768
LAST = 32
MIB = 2**20


def act(pre):
    return jnp.square(jax.nn.relu(pre))


def backward_body(nd, pieces, blocks, chained, *refs):
    refs = refs[1 + chained:]
    dys, pres, (wd, wi), refs = refs[:pieces], refs[pieces:pieces + blocks], refs[pieces + blocks:pieces + blocks + 2], refs[pieces + blocks + 2:]
    dp_out, *t_out = refs[:2] if blocks == 1 else refs[:5]
    dp_all, *dy_all = refs[1 + len(t_out):]
    i = pl.program_id(0)
    rows = dp_out.shape[0] // blocks
    half = rows // 2
    tile = wd.shape[0]
    if pieces == 1:
        dy_all = dys[0]
    else:
        dy_all = dy_all[0]

        @pl.when(i == 0)
        def _():
            at = 0
            for dy in dys:
                dy_all[at:at + dy.shape[0]] = dy[...]
                at += dy.shape[0]

    @pl.when(i < nd)
    def _():
        d_hidden = lax.dot_general(dy_all[...], wd[...], NT, preferred_element_type=F32)
        for k in range(blocks):
            part = slice(k * rows, (k + 1) * rows)
            dp = (d_hidden[part] * (2.0 * jnp.maximum(pres[k][...].astype(F32), 0.0))).astype(BF16)
            dp_out[part] = dp
            dp_all[part, pl.ds(pl.multiple_of(i * tile, tile), tile)] = dp

    @pl.when(i >= nd)
    def _():
        t = lax.dot_general(dp_all[...], wi[...], NT, preferred_element_type=F32)
        if blocks == 1:
            t_out[0][...] = t
        else:
            first_a, first_b, rest_a, rest_b = t_out
            first_a[...] = t[:half].astype(BF16)
            rest_b[...] = t[half:rows]
            rest_a[...] = t[rows:rows + half]
            first_b[...] = t[rows + half:].astype(BF16)


def backward(me, dys, owners, pre, w_in, w_down, place, d_pre=None):
    chained = [] if d_pre is None else [d_pre]
    blocks = len(owners)
    total, d = sum(v.shape[0] for v in dys), dys[0].shape[1]
    rows, ff = total // blocks, pre.shape[1]
    half = rows // 2
    nd, ni = ff // TILE, d // TILE
    phase1 = lambda i: jnp.minimum(i, nd - 1)
    phase2 = lambda i: jnp.maximum(i - nd, 0)

    def pre_spec(k):
        return pl.BlockSpec((rows, TILE), lambda i, o: (lax.rem(o[0] + owners[k], pre.shape[0] // rows), phase1(i)))

    terms = [(rows, F32)] if blocks == 1 else [(half, BF16), (half, BF16), (half, F32), (half, F32)]
    return pl.pallas_call(
        functools.partial(backward_body, nd, len(dys), blocks, len(chained)),
        grid_spec=pltpu.PrefetchScalarGridSpec(
            num_scalar_prefetch=1,
            grid=(nd + ni,),
            in_specs=[pl.BlockSpec(memory_space=pl.ANY)] * len(chained)
            + [pl.BlockSpec(v.shape, lambda i, o: (0, 0)) for v in dys]
            + [pre_spec(k) for k in range(blocks)]
            + [pl.BlockSpec((TILE, d), lambda i, o: (phase1(i), 0)), pl.BlockSpec((TILE, ff), lambda i, o: (phase2(i), 0))],
            out_specs=[pl.BlockSpec((total, TILE), lambda i, o: (place, phase1(i)))]
            + [pl.BlockSpec((r, TILE), lambda i, o: (0, phase2(i))) for r, _ in terms],
            scratch_shapes=[pltpu.VMEM((total, ff), BF16)] + [pltpu.VMEM((total, d), BF16)] * (len(dys) > 1),
        ),
        out_shape=[jax.ShapeDtypeStruct((pre.shape[0], ff), BF16)] + [jax.ShapeDtypeStruct((r, d), t) for r, t in terms],
        input_output_aliases={1: 0} if chained else {},
        compiler_params=pltpu.CompilerParams(vmem_limit_bytes=(36 if blocks == 1 else 48) * MIB, dimension_semantics=("arbitrary",)),
        cost_estimate=pl.CostEstimate(flops=4 * total * d * ff, bytes_accessed=4 * d * ff, transcendentals=0),
    )(me, *chained, *dys, *[pre] * blocks, w_down, w_in)


def most_body(t, s, u, out):
    rows, size = t.shape[0], s.shape[0]
    out[:size] = (t[:size] + s[...].astype(F32)).astype(BF16)
    out[rows - size:] = (t[rows - size:] + u[...].astype(F32)).astype(BF16)


def last_body(t, s, u, _, out):
    size = s.shape[0]
    out[:size] = (t[:size] + s[...].astype(F32)).astype(BF16)
    out[size:] = (t[size:] + u[...].astype(F32)).astype(BF16)


def finish(term, s0, u0, s1, u1):
    rows, d = term.shape
    tn = d // 2
    middle = 2 * s1.shape[0]
    spec = lambda r: pl.BlockSpec((r, tn), lambda j: (0, j))
    params = pltpu.CompilerParams(vmem_limit_bytes=16 * MIB, dimension_semantics=("arbitrary",))
    dx = pl.pallas_call(
        most_body,
        grid=(d // tn,),
        in_specs=[spec(v.shape[0]) for v in (term, s0, u0)],
        out_specs=spec(rows),
        out_shape=pltpu.HBM((rows, d), BF16),
        compiler_params=params,
        cost_estimate=pl.CostEstimate(flops=rows * d, bytes_accessed=8 * rows * d, transcendentals=0),
    )(term, s0, u0)
    place = pl.BlockSpec((pl.Element(middle), pl.Element(d)), lambda i: ((rows - middle) // 2, 0))
    whole = pl.BlockSpec(s1.shape, lambda i: (0, 0))
    return pl.pallas_call(
        last_body,
        grid=(1,),
        in_specs=[place, whole, whole, pl.BlockSpec(memory_space=pl.ANY)],
        out_specs=place,
        out_shape=pltpu.HBM((rows, d), BF16),
        input_output_aliases={3: 0},
        compiler_params=params,
        cost_estimate=pl.CostEstimate(flops=middle * d, bytes_accessed=8 * middle * d, transcendentals=0),
    )(term, s1, u1, dx)


def hidden_body(pre, out):
    out[...] = act(pre[...].astype(F32)).astype(BF16).T


def hidden_transposed(pre):
    rows, ff = pre.shape
    return pl.pallas_call(
        hidden_body,
        grid=(ff // TILE,),
        in_specs=[pl.BlockSpec((rows, TILE), lambda i: (0, i))],
        out_specs=pl.BlockSpec((TILE, rows), lambda i: (i, 0)),
        out_shape=jax.ShapeDtypeStruct((ff, rows), BF16),
        compiler_params=pltpu.CompilerParams(vmem_limit_bytes=24 * MIB, dimension_semantics=("arbitrary",)),
        cost_estimate=pl.CostEstimate(flops=4 * rows * ff, bytes_accessed=4 * rows * ff, transcendentals=0),
    )(pre)


def dw_down_body(pieces, starts, hidden, *refs):
    dys, (out, dy_all) = refs[:pieces], refs[pieces:]

    @pl.when(pl.program_id(1) == 0)
    def _():
        for k, dy in enumerate(dys):
            size = dy.shape[0]
            dy_all[pl.ds(pl.multiple_of(starts(k), 16), size)] = dy[...]

    out[...] = jnp.dot(hidden[...], dy_all[...], preferred_element_type=F32).astype(BF16)


def grad_w_down(me, hidden, starts, block, dys):
    ff, rows = hidden.shape
    d = dys[0].shape[1]
    m, tn = ff // 2, d // 3

    def body(me, *refs):
        def start(k):
            owner, row = starts[k]
            return lax.rem(me[0] + owner, rows // block) * block + row

        return dw_down_body(len(dys), start, *refs)

    return pl.pallas_call(
        body,
        grid_spec=pltpu.PrefetchScalarGridSpec(
            num_scalar_prefetch=1,
            grid=(d // tn, ff // m),
            in_specs=[pl.BlockSpec((m, rows), lambda j, i, o: (i, 0))]
            + [pl.BlockSpec((v.shape[0], tn), lambda j, i, o: (0, j)) for v in dys],
            out_specs=pl.BlockSpec((m, tn), lambda j, i, o: (i, j)),
            scratch_shapes=[pltpu.VMEM((rows, tn), BF16)],
        ),
        out_shape=jax.ShapeDtypeStruct((ff, d), BF16),
        compiler_params=pltpu.CompilerParams(vmem_limit_bytes=32 * MIB, dimension_semantics=("arbitrary", "arbitrary")),
        cost_estimate=pl.CostEstimate(flops=2 * rows * ff * d, bytes_accessed=2 * (rows * ff + 2 * rows * d + ff * d), transcendentals=0),
    )(me, hidden, *dys)


def dw_in_body(columns, *refs):
    pieces = len(columns)
    xs, d_pre, (out, x_all, sems) = refs[:pieces], refs[pieces], refs[-3:]

    @pl.when(pl.program_id(0) == 0)
    def _():
        copies, at = [], 0
        for k, (x, c) in enumerate(zip(xs, columns)):
            src = x.at[:, pl.ds(c, x_all.shape[1])]
            copies.append(pltpu.make_async_copy(src, x_all.at[pl.ds(at, x.shape[0])], sems.at[k]))
            at += x.shape[0]
        for copy in copies:
            copy.start()
        for copy in copies:
            copy.wait()

    out[...] = lax.dot_general(x_all[...], d_pre[...], TN, preferred_element_type=F32).astype(BF16)


def grad_w_in(xs, d_pre, part, d, out=None):
    rows, ff = d_pre.shape
    m, tn = d // 2, TILE
    columns = [part * m if x.shape[1] == d else 0 for x in xs]
    chained = [] if out is None else [out]
    return pl.pallas_call(
        functools.partial(dw_in_body, columns),
        grid=(ff // tn,),
        in_specs=[pl.BlockSpec(memory_space=pl.ANY)] * len(xs)
        + [pl.BlockSpec((rows, tn), lambda i: (0, i))]
        + [pl.BlockSpec(memory_space=pl.ANY)] * len(chained),
        out_specs=pl.BlockSpec((m, tn), lambda i: (part, i)),
        scratch_shapes=[pltpu.VMEM((rows, m), BF16), pltpu.SemaphoreType.DMA((len(xs),))],
        out_shape=jax.ShapeDtypeStruct((d, ff), BF16),
        input_output_aliases={len(xs) + 1: 0} if chained else {},
        compiler_params=pltpu.CompilerParams(vmem_limit_bytes=26 * MIB, dimension_semantics=("arbitrary",)),
        cost_estimate=pl.CostEstimate(flops=2 * rows * m * ff, bytes_accessed=2 * (rows * m + rows * ff + m * ff), transcendentals=0),
    )(*xs, d_pre, *chained)


def solution(mesh):
    n = mesh.shape["tp"]
    right = [(i, (i + 1) % n) for i in range(n)]
    left = [(i, (i - 1) % n) for i in range(n)]

    def send(a, b):
        a = lax.ppermute(a, "tp", right)
        b = lax.ppermute(b, "tp", left)
        return a, b

    def add(term, got):
        return (term + got.astype(F32)).astype(BF16)

    def step(x, dy, pre, w_in, w_down):
        me = lax.axis_index("tp").reshape(1)
        rows, d = x.shape
        half, m = rows // 2, d // 2
        lo, ro, own, oo = n - 1, 1, 0, 2

        dy_lo, dy_ro = send(dy, dy)
        x_lot, x_rob = send(x[:half], x[half:])
        d_pre, t0 = backward(me, [dy], [own], pre, w_in, w_down, 2)
        hidden = hidden_transposed(pre)
        dy_ot, dy_ob = send(dy_lo[:half], dy_ro[half:])
        d_pre, s, u, rest_a, rest_b = backward(me, [dy_lo, dy_ro], [lo, ro], pre, w_in, w_down, 0, d_pre)
        s, u = send(s, u)
        x_lob, x_rot = send(x[half:], x[:half])
        x_ota, x_oba = send(x_lot[:, :m], x_rob[:, :m])
        d_pre, t3 = backward(me, [dy_ot, dy_ob], [oo], pre, w_in, w_down, 3, d_pre)
        s, u = send(add(t3[:half], s), add(t3[half:], u))
        x_otb, x_obb = send(x_lot[:, m:], x_rob[:, m:])
        starts = [(lo, 0), (ro, 0), (own, 0), (oo, 0), (oo, half)]
        dw_down = grad_w_down(me, hidden, starts, rows, [dy_lo, dy_ro, dy, dy_ot, dy_ob])
        dw_in = grad_w_in([x_lot, x_lob, x_rot, x_rob, x, x_ota, x_oba], d_pre, 0, d)
        c = half - LAST
        s0, u0 = send(add(rest_a[:c], s[:c]), add(rest_b[LAST:], u[LAST:]))
        s1, u1 = send(add(rest_a[c:], s[c:]), add(rest_b[:LAST], u[:LAST]))
        dw_in = grad_w_in([x_lot, x_lob, x_rot, x_rob, x, x_otb, x_obb], d_pre, 1, d, dw_in)
        dx = finish(t0, s0, u0, s1, u1)
        return dx, dw_in, dw_down

    tokens = P(("dp", "tp"), None)
    return jax.shard_map(
        step,
        mesh=mesh,
        in_specs=(tokens, tokens, P("dp", "tp"), P(None, "tp"), P("tp", None)),
        out_specs=(tokens, P("dp", "tp"), tokens),
        check_vma=False,
    )
```

profile of v0, /device:TPU:112, one launch (start us, length us, event | category | flops | bytes accessed | tf_op | source)
XLA Modules:
  0.0 246.3 jit_solution(5418691923722946640)
XLA Ops:
  0.6 2.4 collective-permute-start
  3.1 1.6 collective-permute-start.1
  4.7 3.0 %fusion = (bf16[176,3072]{1,0:T(8,128)(2,1)}, bf16[176,3072]{1,0:T(8,128)(2,1)}) fusion(bf16[352,3072]{1,0:T(8,128)(2,1)} %refs_4_.9), kind=kLoop, calls=%fused_computation.6 | loop fusion | bytes 4325376 | tf_op jit(solution)/shard_map/slice | solution.py:262
  7.7 0.4 collective-permute-start.12
  8.1 1.6 collective-permute-start.13
  9.7 1.6 collective-permute-start.15
  11.3 2.8 %copy-done = bf16[1408,2304]{1,0:T(8,128)(2,1)S(1)} copy-done((bf16[1408,2304]{1,0:T(8,128)(2,1)S(1)}, bf16[1408,2304]{1,0:T(8,128)(2,1)}, u32[]{:S(2)}) %copy-start) | copy-done | bytes 6488088
  14.2 2.3 shard_map.83.refs_0_
  16.5 2.7 %copy-done.6 = bf16[2304,1408]{1,0:T(8,128)(2,1)} copy-done((bf16[2304,1408]{1,0:T(8,128)(2,1)}, bf16[2304,1408]{1,0:T(8,128)(2,1)S(1)}, u32[]{:S(2)}) %copy-start.6) | copy-done | bytes 6488088
  19.3 17.2 %shard_map.76 = (bf16[1408,2304]{1,0:T(8,128)(2,1)S(1)}, f32[352,3072]{1,0:T(8,128)S(1)}) custom-call(s32[1]{0:T(128)} %bitcast.refs_0_.me, bf16[352,3072]{1,0:T(8,128)(2,1)S(1)} %copy-done.8, bf16[1408,2304]{1,0:T(8,128)(2,1)} %pre.1, bf16[2304,3072]{1,0:T(8,128)(2,1)} %refs_5_.3, bf16[3072,2304]{1,0:T(8,128)(2,1)} %refs_6_.3), custom_call_target="tpu_custom_call" | custom-call | flops 9965666304 | bytes 28311552 | tf_op jit(solution)/shard_map/pallas_call | solution.py:79
  36.5 2.8 %copy-done.1 = bf16[1408,2304]{1,0:T(8,128)(2,1)} copy-done((bf16[1408,2304]{1,0:T(8,128)(2,1)}, bf16[1408,2304]{1,0:T(8,128)(2,1)S(1)}, u32[]{:S(2)}) %copy-start.1) | copy-done | bytes 6488088
  39.2 36.7 %collective-permute-done.12.refs_0_ = bf16[176,3072]{1,0:T(8,128)(2,1)S(1)} collective-permute-done((bf16[176,3072]{1,0:T(8,128)(2,1)}, bf16[176,3072]{1,0:T(8,128)(2,1)S(1)}, u32[]{:S(2)}, u32[]{:S(2)}) %collective-permute-start.12) | collective-permute-done | bytes 1081376 | tf_op jit(solution)/shard_map/ppermute | solution.py:242
  75.9 1.0 fusion.2
  76.9 1.3 slice.74
  78.2 0.5 collective-permute-start.2
  78.8 2.3 slice.75
  81.1 2.8 %collective-permute-start.3 = (bf16[176,3072]{1,0:T(8,128)(2,1)}, bf16[176,3072]{1,0:T(8,128)(2,1)S(1)}, u32[]{:S(2)}, u32[]{:S(2)}) collective-permute-start(bf16[176,3072]{1,0:T(8,128)(2,1)} %slice.75), channel_id=1, source_target_pairs={{0,3},{1,0},{2,1},{3,2},{4,7},{5,4},{6,5},{7,6},{8,11},{9,8},{10,9... | collective-permute-start | bytes 3244040 | tf_op jit(solution)/shard_map/ppermute | solution.py:243
  83.8 29.0 %shard_map.77 = (bf16[1408,2304]{1,0:T(8,128)(2,1)}, bf16[176,3072]{1,0:T(8,128)(2,1)}, bf16[176,3072]{1,0:T(8,128)(2,1)S(1)}, f32[176,3072]{1,0:T(8,128)S(1)}, f32[176,3072]{1,0:T(8,128)}) custom-call(s32[1]{0:T(128)} %bitcast.refs_0_.me, bf16[1408,2304]{1,0:T(8,128)(2,1)} %copy-done.1, ...), custom_call_target="tpu_custom_call", output_to_operand_aliasing={{0}: (1, {})} | custom-call | flops 19931332608 | bytes 28311552 | tf_op jit(solution)/shard_map/pallas_call | solution.py:79
  112.8 0.9 collective-permute-start.7
  113.7 1.2 collective-permute-start.4
  115.0 1.1 fusion.1
  116.0 6.2 %collective-permute-done.2.refs_2_.refs_4_ = bf16[176,3072]{1,0:T(8,128)(2,1)S(1)} collective-permute-done((bf16[176,3072]{1,0:T(8,128)(2,1)S(1)}, bf16[176,3072]{1,0:T(8,128)(2,1)S(1)}, u32[]{:S(2)}, u32[]{:S(2)}) %collective-permute-start.2) | collective-permute-done | bytes 1081376 | tf_op jit(solution)/shard_map/ppermute | solution.py:242
  122.2 2.0 collective-permute-start.14
  124.2 0.0 collective-permute-start.18
  124.3 3.2 %copy-done.2 = bf16[1408,2304]{1,0:T(8,128)(2,1)S(1)} copy-done((bf16[1408,2304]{1,0:T(8,128)(2,1)S(1)}, bf16[1408,2304]{1,0:T(8,128)(2,1)}, u32[]{:S(2)}) %copy-start.2) | copy-done | bytes 6488088
  127.5 17.3 %shard_map.78 = (bf16[1408,2304]{1,0:T(8,128)(2,1)S(1)}, f32[352,3072]{1,0:T(8,128)S(1)}) custom-call(s32[1]{0:T(128)} %bitcast.refs_0_.me, bf16[1408,2304]{1,0:T(8,128)(2,1)S(1)} %copy-done.2, bf16[176,3072]{1,0:T(8,128)(2,1)S(1)} %collective-permute-done.2.refs_2_.refs_4_, ...), custom_call_target="tpu_custom_call", output_to_operand_aliasing={{0}: (1, {})} | custom-call | flops 9965666304 | bytes 28311552 | tf_op jit(solution)/shard_map/pallas_call | solution.py:79
  144.8 2.9 %collective-permute-start.19 = (bf16[176,1536]{1,0:T(8,128)(2,1)}, bf16[176,1536]{1,0:T(8,128)(2,1)}, u32[]{:S(2)}, u32[]{:S(2)}) collective-permute-start(bf16[176,1536]{1,0:T(8,128)(2,1)} %get-tuple-element.25), channel_id=1, source_target_pairs={{0,3},{1,0},{2,1},{3,2},{4,7},{5,4},{6,5},{7,6},{8,11},{9,8},{10,9... | collective-permute-start | bytes 1622024 | tf_op jit(solution)/shard_map/ppermute | solution.py:243
  147.7 2.0 add_convert_fusion
  149.8 3.0 %copy-done.7 = bf16[2304,1408]{1,0:T(8,128)(2,1)S(1)} copy-done((bf16[2304,1408]{1,0:T(8,128)(2,1)S(1)}, bf16[2304,1408]{1,0:T(8,128)(2,1)}, u32[]{:S(2)}) %copy-start.7) | copy-done | bytes 6488088
  152.8 2.0 copy-done.13
  154.8 1.2 copy-done.15
  156.1 27.0 %shard_map.84 = bf16[2304,3072]{1,0:T(8,128)(2,1)} custom-call(s32[1]{0:T(128)} %bitcast.refs_0_.me, bf16[2304,1408]{1,0:T(8,128)(2,1)S(1)} %copy-done.7, bf16[352,3072]{1,0:T(8,128)(2,1)} %collective-permute-done.refs_2_.refs_1_, bf16[352,3072]{1,0:T(8,128)(2,1)} %collective-permute-done.1.refs_3_.refs_2_, bf16[352,3072]{1,0:T(8,128)(2,1)S(1)} %copy-done.9, ...), custom_call_target="tpu_custom_call" | custom-call | flops 19931332608 | bytes 37945344 | tf_op jit(solution)/shard_map/pallas_call | solution.py:181
  183.0 3.2 %collective-permute-start.17 = (bf16[176,1536]{1,0:T(8,128)(2,1)}, bf16[176,1536]{1,0:T(8,128)(2,1)S(1)}, u32[]{:S(2)}, u32[]{:S(2)}) collective-permute-start(bf16[176,1536]{1,0:T(8,128)(2,1)} %get-tuple-element.26), channel_id=1, source_target_pairs={{0,3},{1,0},{2,1},{3,2},{4,7},{5,4},{6,5},{7,6},{8,11},{9,8},{10,9... | collective-permute-start | bytes 1622024 | tf_op jit(solution)/shard_map/ppermute | solution.py:243
  186.3 1.8 collective-permute-start.8
  188.1 15.4 %shard_map.81.refs_8_ = bf16[3072,2304]{1,0:T(8,128)(2,1)} custom-call(bf16[176,3072]{1,0:T(8,128)(2,1)S(1)} %collective-permute-done.12.refs_0_, bf16[176,3072]{1,0:T(8,128)(2,1)S(1)} %collective-permute-done.13.refs_1_, bf16[176,3072]{1,0:T(8,128)(2,1)S(1)} %collective-permute-done.14.refs_2_, bf16[176,3072]{1,0:T(8,128)(2,1)S(1)} %collective-permute-done.15.refs_3_, ...), custom_call_target="tpu_custom_call" | custom-call | flops 9965666304 | bytes 17891328 | tf_op jit(solution)/shard_map/pallas_call | solution.py:221
  203.5 1.0 add_convert_fusion.5
  204.4 0.4 collective-permute-start.6
  204.8 13.8 %collective-permute-done.8 = bf16[176,3072]{1,0:T(8,128)(2,1)S(1)} collective-permute-done((bf16[176,3072]{1,0:T(8,128)(2,1)}, bf16[176,3072]{1,0:T(8,128)(2,1)S(1)}, u32[]{:S(2)}, u32[]{:S(2)}) %collective-permute-start.8) | collective-permute-done | bytes 1081376 | tf_op jit(solution)/shard_map/ppermute | solution.py:243
  218.7 3.4 %collective-permute-start.9 = (bf16[32,3072]{1,0:T(8,128)(2,1)S(1)}, bf16[32,3072]{1,0:T(8,128)(2,1)S(1)}, u32[]{:S(2)}, u32[]{:S(2)}) collective-permute-start(bf16[32,3072]{1,0:T(8,128)(2,1)S(1)} %add_convert_fusion.4), channel_id=1, source_target_pairs={{0,3},{1,0},{2,1},{3,2},{4,7},{5,4},{6,5},{7,6},{8,11},{9,8},{10,9... | collective-permute-start | bytes 589832 | tf_op jit(solution)/shard_map/ppermute | solution.py:243
  222.1 1.3 add_convert_fusion.3
  223.4 0.1 collective-permute-start.10
  223.5 0.2 add_convert_fusion.2
  223.7 3.3 %collective-permute-start.11 = (bf16[144,3072]{1,0:T(8,128)(2,1)S(1)}, bf16[144,3072]{1,0:T(8,128)(2,1)S(1)}, u32[]{:S(2)}, u32[]{:S(2)}) collective-permute-start(bf16[144,3072]{1,0:T(8,128)(2,1)S(1)} %add_convert_fusion.2), channel_id=1, source_target_pairs={{0,3},{1,0},{2,1},{3,2},{4,7},{5,4},{6,5},{7,6},{8,11},{9,8},{10,9... | collective-permute-start | bytes 2654216 | tf_op jit(solution)/shard_map/ppermute | solution.py:243
  227.0 14.0 %shard_map.82 = bf16[3072,2304]{1,0:T(8,128)(2,1)} custom-call(bf16[176,3072]{1,0:T(8,128)(2,1)S(1)} %collective-permute-done.12.refs_0_, bf16[176,3072]{1,0:T(8,128)(2,1)S(1)} %collective-permute-done.13.refs_1_, bf16[176,3072]{1,0:T(8,128)(2,1)S(1)} %collective-permute-done.14.refs_2_, ...), custom_call_target="tpu_custom_call", output_to_operand_aliasing={{}: (8, {})} | custom-call | flops 9965666304 | bytes 17891328 | tf_op jit(solution)/shard_map/pallas_call | solution.py:221
  241.0 0.9 collective-permute-done.10.s
  241.9 1.6 collective-permute-done.11.u
  243.6 1.9 shard_map.79._
  245.5 0.8 shard_map.80
  (45 shorter events, 0.2 us)
Async XLA Ops:
  0.6 76.3 %collective-permute-start = (bf16[352,3072]{1,0:T(8,128)(2,1)}, bf16[352,3072]{1,0:T(8,128)(2,1)}, u32[]{:S(2)}, u32[]{:S(2)}) collective-permute-start(bf16[352,3072]{1,0:T(8,128)(2,1)} %refs_3_.3), channel_id=1, source_target_pairs={{0,1},{1,2},{2,3},{3,0},{4,5},{5,6},{6,7},{7,4},{8,9},{9,10},{10,1... | collective-permute-start | bytes 6488072 | tf_op jit(solution)/shard_map/ppermute | solution.py:242
  3.1 75.7 %collective-permute-start.1 = (bf16[352,3072]{1,0:T(8,128)(2,1)}, bf16[352,3072]{1,0:T(8,128)(2,1)}, u32[]{:S(2)}, u32[]{:S(2)}) collective-permute-start(bf16[352,3072]{1,0:T(8,128)(2,1)} %refs_3_.3), channel_id=1, source_target_pairs={{0,3},{1,0},{2,1},{3,2},{4,7},{5,4},{6,5},{7,6},{8,11},{9,8},{10,9... | collective-permute-start | bytes 6488072 | tf_op jit(solution)/shard_map/ppermute | solution.py:243
  7.7 68.1 %collective-permute-start.12 = (bf16[176,3072]{1,0:T(8,128)(2,1)}, bf16[176,3072]{1,0:T(8,128)(2,1)S(1)}, u32[]{:S(2)}, u32[]{:S(2)}) collective-permute-start(bf16[176,3072]{1,0:T(8,128)(2,1)} %get-tuple-element.24), channel_id=1, source_target_pairs={{0,1},{1,2},{2,3},{3,0},{4,5},{5,6},{6,7},{7,4},{8,9},{9,10},{10,1... | collective-permute-start | bytes 3244040 | tf_op jit(solution)/shard_map/ppermute | solution.py:242
  8.1 174.9 %collective-permute-start.13 = (bf16[176,3072]{1,0:T(8,128)(2,1)}, bf16[176,3072]{1,0:T(8,128)(2,1)S(1)}, u32[]{:S(2)}, u32[]{:S(2)}) collective-permute-start(bf16[176,3072]{1,0:T(8,128)(2,1)} %get-tuple-element.23), channel_id=1, source_target_pairs={{0,1},{1,2},{2,3},{3,0},{4,5},{5,6},{6,7},{7,4},{8,9},{9,10},{10,1... | collective-permute-start | bytes 3244040 | tf_op jit(solution)/shard_map/ppermute | solution.py:242
  9.7 104.0 %collective-permute-start.15 = (bf16[176,3072]{1,0:T(8,128)(2,1)}, bf16[176,3072]{1,0:T(8,128)(2,1)S(1)}, u32[]{:S(2)}, u32[]{:S(2)}) collective-permute-start(bf16[176,3072]{1,0:T(8,128)(2,1)} %get-tuple-element.23), channel_id=1, source_target_pairs={{0,3},{1,0},{2,1},{3,2},{4,7},{5,4},{6,5},{7,6},{8,11},{9,8},{10,9... | collective-permute-start | bytes 3244040 | tf_op jit(solution)/shard_map/ppermute | solution.py:243
  11.3 2.8 %copy-start = (bf16[1408,2304]{1,0:T(8,128)(2,1)S(1)}, bf16[1408,2304]{1,0:T(8,128)(2,1)}, u32[]{:S(2)}) copy-start(bf16[1408,2304]{1,0:T(8,128)(2,1)} %pre.1) | copy-start | bytes 19464196
  14.2 5.1 %copy-start.8 = (bf16[352,3072]{1,0:T(8,128)(2,1)S(1)}, bf16[352,3072]{1,0:T(8,128)(2,1)}, u32[]{:S(2)}) copy-start(bf16[352,3072]{1,0:T(8,128)(2,1)} %refs_3_.3) | copy-start | bytes 6488068
  16.5 2.7 %copy-start.6 = (bf16[2304,1408]{1,0:T(8,128)(2,1)}, bf16[2304,1408]{1,0:T(8,128)(2,1)S(1)}, u32[]{:S(2)}) copy-start(bf16[2304,1408]{1,0:T(8,128)(2,1)S(1)} %shard_map.83.refs_0_) | copy-start | bytes 19464196
  36.4 2.8 %copy-start.1 = (bf16[1408,2304]{1,0:T(8,128)(2,1)}, bf16[1408,2304]{1,0:T(8,128)(2,1)S(1)}, u32[]{:S(2)}) copy-start(bf16[1408,2304]{1,0:T(8,128)(2,1)S(1)} %get-tuple-element.13.refs_1_) | copy-start | bytes 19464196
  78.2 44.0 %collective-permute-start.2 = (bf16[176,3072]{1,0:T(8,128)(2,1)S(1)}, bf16[176,3072]{1,0:T(8,128)(2,1)S(1)}, u32[]{:S(2)}, u32[]{:S(2)}) collective-permute-start(bf16[176,3072]{1,0:T(8,128)(2,1)S(1)} %slice.74), channel_id=1, source_target_pairs={{0,1},{1,2},{2,3},{3,0},{4,5},{5,6},{6,7},{7,4},{8,9},{9,10},{10,1... | collective-permute-start | bytes 3244040 | tf_op jit(solution)/shard_map/ppermute | solution.py:242
  81.1 43.2 %collective-permute-start.3 = (bf16[176,3072]{1,0:T(8,128)(2,1)}, bf16[176,3072]{1,0:T(8,128)(2,1)S(1)}, u32[]{:S(2)}, u32[]{:S(2)}) collective-permute-start(bf16[176,3072]{1,0:T(8,128)(2,1)} %slice.75), channel_id=1, source_target_pairs={{0,3},{1,0},{2,1},{3,2},{4,7},{5,4},{6,5},{7,6},{8,11},{9,8},{10,9... | collective-permute-start | bytes 3244040 | tf_op jit(solution)/shard_map/ppermute | solution.py:243
  112.8 31.9 %copy-start.10 = (f32[176,3072]{1,0:T(8,128)}, f32[176,3072]{1,0:T(8,128)S(1)}, u32[]{:S(2)}) copy-start(f32[176,3072]{1,0:T(8,128)S(1)} %get-tuple-element.14) | copy-start | bytes 6488068
  112.8 32.0 %collective-permute-start.7 = (bf16[176,3072]{1,0:T(8,128)(2,1)S(1)}, bf16[176,3072]{1,0:T(8,128)(2,1)S(1)}, u32[]{:S(2)}, u32[]{:S(2)}) collective-permute-start(bf16[176,3072]{1,0:T(8,128)(2,1)S(1)} %get-tuple-element.19), channel_id=1, source_target_pairs={{0,3},{1,0},{2,1},{3,2},{4,7},{5,4},{6,5},{7,6},{8,11},{9,8},{10,9... | collective-permute-start | bytes 3244040 | tf_op jit(solution)/shard_map/ppermute | solution.py:243
  113.7 34.0 %collective-permute-start.4 = (bf16[176,3072]{1,0:T(8,128)(2,1)}, bf16[176,3072]{1,0:T(8,128)(2,1)S(1)}, u32[]{:S(2)}, u32[]{:S(2)}) collective-permute-start(bf16[176,3072]{1,0:T(8,128)(2,1)} %get-tuple-element.17), channel_id=1, source_target_pairs={{0,1},{1,2},{2,3},{3,0},{4,5},{5,6},{6,7},{7,4},{8,9},{9,10},{10,1... | collective-permute-start | bytes 3244040 | tf_op jit(solution)/shard_map/ppermute | solution.py:242
  122.2 22.6 %copy-start.12 = (bf16[176,3072]{1,0:T(8,128)(2,1)}, bf16[176,3072]{1,0:T(8,128)(2,1)S(1)}, u32[]{:S(2)}) copy-start(bf16[176,3072]{1,0:T(8,128)(2,1)S(1)} %collective-permute-done.2.refs_2_.refs_4_) | copy-start | bytes 3244036
  122.2 60.8 %collective-permute-start.14 = (bf16[176,3072]{1,0:T(8,128)(2,1)}, bf16[176,3072]{1,0:T(8,128)(2,1)S(1)}, u32[]{:S(2)}, u32[]{:S(2)}) collective-permute-start(bf16[176,3072]{1,0:T(8,128)(2,1)} %get-tuple-element.24), channel_id=1, source_target_pairs={{0,3},{1,0},{2,1},{3,2},{4,7},{5,4},{6,5},{7,6},{8,11},{9,8},{10,9... | collective-permute-start | bytes 3244040 | tf_op jit(solution)/shard_map/ppermute | solution.py:243
  124.2 20.6 %copy-start.14 = (bf16[176,3072]{1,0:T(8,128)(2,1)}, bf16[176,3072]{1,0:T(8,128)(2,1)S(1)}, u32[]{:S(2)}) copy-start(bf16[176,3072]{1,0:T(8,128)(2,1)S(1)} %collective-permute-done.3.refs_3_.refs_5_) | copy-start | bytes 3244036
  124.2 62.0 %collective-permute-start.18 = (bf16[176,1536]{1,0:T(8,128)(2,1)}, bf16[176,1536]{1,0:T(8,128)(2,1)}, u32[]{:S(2)}, u32[]{:S(2)}) collective-permute-start(bf16[176,1536]{1,0:T(8,128)(2,1)} %get-tuple-element.27), channel_id=1, source_target_pairs={{0,1},{1,2},{2,3},{3,0},{4,5},{5,6},{6,7},{7,4},{8,9},{9,10},{10,1... | collective-permute-start | bytes 1622024 | tf_op jit(solution)/shard_map/ppermute | solution.py:242
  124.3 3.2 %copy-start.2 = (bf16[1408,2304]{1,0:T(8,128)(2,1)S(1)}, bf16[1408,2304]{1,0:T(8,128)(2,1)}, u32[]{:S(2)}) copy-start(bf16[1408,2304]{1,0:T(8,128)(2,1)} %get-tuple-element.15.refs_1_) | copy-start | bytes 19464196
  144.8 5.0 %copy-start.3 = (bf16[1408,2304]{1,0:T(8,128)(2,1)}, bf16[1408,2304]{1,0:T(8,128)(2,1)S(1)}, u32[]{:S(2)}) copy-start(bf16[1408,2304]{1,0:T(8,128)(2,1)S(1)} %get-tuple-element.20.refs_7_) | copy-start | bytes 19464196
  144.8 43.2 %collective-permute-start.19 = (bf16[176,1536]{1,0:T(8,128)(2,1)}, bf16[176,1536]{1,0:T(8,128)(2,1)}, u32[]{:S(2)}, u32[]{:S(2)}) collective-permute-start(bf16[176,1536]{1,0:T(8,128)(2,1)} %get-tuple-element.25), channel_id=1, source_target_pairs={{0,3},{1,0},{2,1},{3,2},{4,7},{5,4},{6,5},{7,6},{8,11},{9,8},{10,9... | collective-permute-start | bytes 1622024 | tf_op jit(solution)/shard_map/ppermute | solution.py:243
  147.7 2.1 copy-start.9
  149.8 38.2 %copy-start.4 = (bf16[1408,2304]{1,0:T(8,128)(2,1)S(1)}, bf16[1408,2304]{1,0:T(8,128)(2,1)}, u32[]{:S(2)}) copy-start(bf16[1408,2304]{1,0:T(8,128)(2,1)} %copy-done.3) | copy-start | bytes 19464196
  149.8 38.2 %copy-start.5 = (bf16[352,3072]{1,0:T(8,128)(2,1)S(1)}, bf16[352,3072]{1,0:T(8,128)(2,1)}, u32[]{:S(2)}) copy-start(bf16[352,3072]{1,0:T(8,128)(2,1)} %refs_4_.9) | copy-start | bytes 6488068
  149.8 53.7 %collective-permute-start.5 = (bf16[176,3072]{1,0:T(8,128)(2,1)}, bf16[176,3072]{1,0:T(8,128)(2,1)}, u32[]{:S(2)}, u32[]{:S(2)}) collective-permute-start(bf16[176,3072]{1,0:T(8,128)(2,1)} %get-tuple-element.22), channel_id=1, source_target_pairs={{0,1},{1,2},{2,3},{3,0},{4,5},{5,6},{6,7},{7,4},{8,9},{9,10},{10,1... | collective-permute-start | bytes 3244040 | tf_op jit(solution)/shard_map/ppermute | solution.py:242
  149.8 3.0 %copy-start.7 = (bf16[2304,1408]{1,0:T(8,128)(2,1)S(1)}, bf16[2304,1408]{1,0:T(8,128)(2,1)}, u32[]{:S(2)}) copy-start(bf16[2304,1408]{1,0:T(8,128)(2,1)} %copy-done.6) | copy-start | bytes 19464196
  152.8 2.0 copy-start.13
  154.8 1.2 copy-start.15
  183.0 40.7 %collective-permute-start.16 = (bf16[176,1536]{1,0:T(8,128)(2,1)}, bf16[176,1536]{1,0:T(8,128)(2,1)S(1)}, u32[]{:S(2)}, u32[]{:S(2)}) collective-permute-start(bf16[176,1536]{1,0:T(8,128)(2,1)} %get-tuple-element.28), channel_id=1, source_target_pairs={{0,1},{1,2},{2,3},{3,0},{4,5},{5,6},{6,7},{7,4},{8,9},{9,10},{10,1... | collective-permute-start | bytes 1622024 | tf_op jit(solution)/shard_map/ppermute | solution.py:242
  183.0 44.0 %collective-permute-start.17 = (bf16[176,1536]{1,0:T(8,128)(2,1)}, bf16[176,1536]{1,0:T(8,128)(2,1)S(1)}, u32[]{:S(2)}, u32[]{:S(2)}) collective-permute-start(bf16[176,1536]{1,0:T(8,128)(2,1)} %get-tuple-element.26), channel_id=1, source_target_pairs={{0,3},{1,0},{2,1},{3,2},{4,7},{5,4},{6,5},{7,6},{8,11},{9,8},{10,9... | collective-permute-start | bytes 1622024 | tf_op jit(solution)/shard_map/ppermute | solution.py:243
  186.3 32.3 %collective-permute-start.8 = (bf16[176,3072]{1,0:T(8,128)(2,1)}, bf16[176,3072]{1,0:T(8,128)(2,1)S(1)}, u32[]{:S(2)}, u32[]{:S(2)}) collective-permute-start(bf16[176,3072]{1,0:T(8,128)(2,1)} %get-tuple-element.21), channel_id=1, source_target_pairs={{0,3},{1,0},{2,1},{3,2},{4,7},{5,4},{6,5},{7,6},{8,11},{9,8},{10,9... | collective-permute-start | bytes 3244040 | tf_op jit(solution)/shard_map/ppermute | solution.py:243
  188.0 15.4 %copy-start.11 = (f32[176,3072]{1,0:T(8,128)S(1)}, f32[176,3072]{1,0:T(8,128)}, u32[]{:S(2)}) copy-start(f32[176,3072]{1,0:T(8,128)} %copy-done.10) | copy-start | bytes 6488068
  188.0 30.6 %copy-start.16 = (f32[176,3072]{1,0:T(8,128)S(1)}, f32[176,3072]{1,0:T(8,128)}, u32[]{:S(2)}) copy-start(f32[176,3072]{1,0:T(8,128)} %get-tuple-element.18) | copy-start | bytes 6488068
  204.4 41.0 %collective-permute-start.6 = (bf16[32,3072]{1,0:T(8,128)(2,1)S(1)}, bf16[32,3072]{1,0:T(8,128)(2,1)S(1)}, u32[]{:S(2)}, u32[]{:S(2)}) collective-permute-start(bf16[32,3072]{1,0:T(8,128)(2,1)S(1)} %add_convert_fusion.5), channel_id=1, source_target_pairs={{0,1},{1,2},{2,3},{3,0},{4,5},{5,6},{6,7},{7,4},{8,9},{9,10},{10,1... | collective-permute-start | bytes 589832 | tf_op jit(solution)/shard_map/ppermute | solution.py:242
  218.7 26.8 %collective-permute-start.9 = (bf16[32,3072]{1,0:T(8,128)(2,1)S(1)}, bf16[32,3072]{1,0:T(8,128)(2,1)S(1)}, u32[]{:S(2)}, u32[]{:S(2)}) collective-permute-start(bf16[32,3072]{1,0:T(8,128)(2,1)S(1)} %add_convert_fusion.4), channel_id=1, source_target_pairs={{0,3},{1,0},{2,1},{3,2},{4,7},{5,4},{6,5},{7,6},{8,11},{9,8},{10,9... | collective-permute-start | bytes 589832 | tf_op jit(solution)/shard_map/ppermute | solution.py:243
  223.4 18.5 %collective-permute-start.10 = (bf16[144,3072]{1,0:T(8,128)(2,1)S(1)}, bf16[144,3072]{1,0:T(8,128)(2,1)S(1)}, u32[]{:S(2)}, u32[]{:S(2)}) collective-permute-start(bf16[144,3072]{1,0:T(8,128)(2,1)S(1)} %add_convert_fusion.3), channel_id=1, source_target_pairs={{0,1},{1,2},{2,3},{3,0},{4,5},{5,6},{6,7},{7,4},{8,9},{9,10},{10,1... | collective-permute-start | bytes 2654216 | tf_op jit(solution)/shard_map/ppermute | solution.py:242
  223.7 19.8 %collective-permute-start.11 = (bf16[144,3072]{1,0:T(8,128)(2,1)S(1)}, bf16[144,3072]{1,0:T(8,128)(2,1)S(1)}, u32[]{:S(2)}, u32[]{:S(2)}) collective-permute-start(bf16[144,3072]{1,0:T(8,128)(2,1)S(1)} %add_convert_fusion.2), channel_id=1, source_target_pairs={{0,3},{1,0},{2,1},{3,2},{4,7},{5,4},{6,5},{7,6},{8,11},{9,8},{10,9... | collective-permute-start | bytes 2654216 | tf_op jit(solution)/shard_map/ppermute | solution.py:243
where the time goes:
time: 247 us; the launch traced here: 246 us
  Pallas kernels  125 us (51%)
  waiting for transfers between devices  59.3 us (24%)
  starting transfers between devices  30.2 us (12%)
  local copies, waits for them, and re-layouts  26.6 us (11%)
  other arithmetic  4.55 us (2%)
    pallas_call x3, Pallas kernels, backward(): pl.pallas_call(functools.partial(backward_body, nd, len(dys), blocks, len...  63.4 us
    ppermute x10, waiting for transfers between devices, send(): a = lax.ppermute(a, 'tp', right)  43.8 us
    pallas_call x2, Pallas kernels, grad_w_in(): pl.pallas_call(functools.partial(dw_in_body, columns), grid=(ff // tn,),...  29.4 us
    pallas_call x1, Pallas kernels, grad_w_down(): pl.pallas_call(body, grid_spec=pltpu.PrefetchScalarGridSpec(num_scalar_pr...  27 us
    ppermute x10, starting transfers between devices, send(): b = lax.ppermute(b, 'tp', left)  23.5 us
    unnamed x34, local copies, waits for them, and re-layouts  17.8 us
    ppermute x10, waiting for transfers between devices, send(): b = lax.ppermute(b, 'tp', left)  15.5 us
    ppermute x10, starting transfers between devices, send(): a = lax.ppermute(a, 'tp', right)  6.71 us
  transfers between devices with their start and end apart: 20, of which 5 were waited for; matrix products, arithmetic and copies ran while one was open for 5% of the time, Pallas kernels for 50%

commit v1 on v0

--- a/solution.py
+++ b/solution.py
@@ -45,7 +45,8 @@
         d_hidden = lax.dot_general(dy_all[...], wd[...], NT, preferred_element_type=F32)
         for k in range(blocks):
             part = slice(k * rows, (k + 1) * rows)
-            dp = (d_hidden[part] * (2.0 * jnp.maximum(pres[k][...].astype(F32), 0.0))).astype(BF16)
+            pre = pres[k][...].astype(F32)
+            dp = jnp.where(pre > 0, d_hidden[part] * (2.0 * pre), 0.0).astype(BF16)
             dp_out[part] = dp
             dp_all[part, pl.ds(pl.multiple_of(i * tile, tile), tile)] = dp
 
@@ -89,7 +90,7 @@
             + [pl.BlockSpec((r, TILE), lambda i, o: (0, phase2(i))) for r, _ in terms],
             scratch_shapes=[pltpu.VMEM((total, ff), BF16)] + [pltpu.VMEM((total, d), BF16)] * (len(dys) > 1),
         ),
-        out_shape=[jax.ShapeDtypeStruct((pre.shape[0], ff), BF16)] + [jax.ShapeDtypeStruct((r, d), t) for r, t in terms],
+        out_shape=[pltpu.HBM((pre.shape[0], ff), BF16)] + [jax.ShapeDtypeStruct((r, d), t) for r, t in terms],
         input_output_aliases={1: 0} if chained else {},
         compiler_params=pltpu.CompilerParams(vmem_limit_bytes=(36 if blocks == 1 else 48) * MIB, dimension_semantics=("arbitrary",)),
         cost_estimate=pl.CostEstimate(flops=4 * total * d * ff, bytes_accessed=4 * d * ff, transcendentals=0),
@@ -148,7 +149,7 @@
         grid=(ff // TILE,),
         in_specs=[pl.BlockSpec((rows, TILE), lambda i: (0, i))],
         out_specs=pl.BlockSpec((TILE, rows), lambda i: (i, 0)),
-        out_shape=jax.ShapeDtypeStruct((ff, rows), BF16),
+        out_shape=pltpu.HBM((ff, rows), BF16),
         compiler_params=pltpu.CompilerParams(vmem_limit_bytes=24 * MIB, dimension_semantics=("arbitrary",)),
         cost_estimate=pl.CostEstimate(flops=4 * rows * ff, bytes_accessed=4 * rows * ff, transcendentals=0),
     )(pre)

time: 247 us -> 246 us (level)
  Pallas kernels: 125 us -> 130 us
  local copies, waits for them, and re-layouts: 26.6 us -> 23.6 us
    unnamed x34 -> x50, local copies, waits for them, and re-layouts: 17.8 us -> 14.5 us
  transfers between devices with their start and end apart: 20 -> 20, of which waited for: 5 -> 4; matrix products, arithmetic and copies ran while one was open for 5% -> 5% of each run, Pallas kernels for 50% -> 53%
where the time goes in v1:
time: 246 us; the launch traced here: 245 us
  Pallas kernels  130 us (53%)
  waiting for transfers between devices  58.2 us (24%)
  starting transfers between devices  30.6 us (12%)
  local copies, waits for them, and re-layouts  23.6 us (10%)
    pallas_call x3, Pallas kernels, backward(): pl.pallas_call(functools.partial(backward_body, nd, len(dys), blocks, len...  65 us
    ppermute x10, waiting for transfers between devices, send(): a = lax.ppermute(a, 'tp', right)  42.1 us
    pallas_call x2, Pallas kernels, grad_w_in(): pl.pallas_call(functools.partial(dw_in_body, columns), grid=(ff // tn,),...  30.5 us
    pallas_call x1, Pallas kernels, grad_w_down(): pl.pallas_call(body, grid_spec=pltpu.PrefetchScalarGridSpec(num_scalar_pr...  27.1 us
    ppermute x10, starting transfers between devices, send(): b = lax.ppermute(b, 'tp', left)  22.6 us
    ppermute x10, waiting for transfers between devices, send(): b = lax.ppermute(b, 'tp', left)  16.1 us
    unnamed x50, local copies, waits for them, and re-layouts  14.5 us
    ppermute x10, starting transfers between devices, send(): a = lax.ppermute(a, 'tp', right)  7.92 us
  transfers between devices with their start and end apart: 20, of which 4 were waited for; matrix products, arithmetic and copies ran while one was open for 5% of the time, Pallas kernels for 53%

profile of v1, /device:TPU:112, one launch (start us, length us, event | category | flops | bytes accessed | tf_op | source)
XLA Modules:
  0.0 245.0 jit_solution(15616277408565820422)
XLA Ops:
  0.6 2.4 collective-permute-start
  3.1 1.6 collective-permute-start.1
  4.7 3.2 %fusion = (bf16[176,3072]{1,0:T(8,128)(2,1)}, bf16[176,3072]{1,0:T(8,128)(2,1)}) fusion(bf16[352,3072]{1,0:T(8,128)(2,1)} %refs_4_.9), kind=kLoop, calls=%fused_computation.6 | loop fusion | bytes 4325376 | tf_op jit(solution)/shard_map/slice | solution.py:263
  7.9 0.4 collective-permute-start.12
  8.3 1.6 collective-permute-start.13
  9.9 1.6 collective-permute-start.15
  11.5 2.8 %copy-done = bf16[1408,2304]{1,0:T(8,128)(2,1)S(1)} copy-done((bf16[1408,2304]{1,0:T(8,128)(2,1)S(1)}, bf16[1408,2304]{1,0:T(8,128)(2,1)}, u32[]{:S(2)}) %copy-start) | copy-done | bytes 6488088
  14.3 4.2 %shard_map.83.refs_0_ = bf16[2304,1408]{1,0:T(8,128)(2,1)} custom-call(bf16[1408,2304]{1,0:T(8,128)(2,1)S(1)} %copy-done), custom_call_target="tpu_custom_call" | custom-call | flops 12976128 | bytes 12976128 | tf_op jit(solution)/shard_map/pallas_call | solution.py:147
  18.6 0.9 copy-done.4
  19.5 17.8 %shard_map.76 = (bf16[1408,2304]{1,0:T(8,128)(2,1)}, f32[352,3072]{1,0:T(8,128)S(1)}) custom-call(s32[1]{0:T(128)} %bitcast.refs_0_.me, bf16[352,3072]{1,0:T(8,128)(2,1)S(1)} %copy-done.4, bf16[1408,2304]{1,0:T(8,128)(2,1)S(1)} %bitcast.2, bf16[2304,3072]{1,0:T(8,128)(2,1)} %refs_5_.3, bf16[3072,2304]{1,0:T(8,128)(2,1)} %refs_6_.3), custom_call_target="tpu_custom_call" | custom-call | flops 9965666304 | bytes 28311552 | tf_op jit(solution)/shard_map/pallas_call | solution.py:80
  37.3 2.0 copy-done.1
  39.3 36.6 %collective-permute-done.12.refs_0_ = bf16[176,3072]{1,0:T(8,128)(2,1)S(1)} collective-permute-done((bf16[176,3072]{1,0:T(8,128)(2,1)}, bf16[176,3072]{1,0:T(8,128)(2,1)S(1)}, u32[]{:S(2)}, u32[]{:S(2)}) %collective-permute-start.12) | collective-permute-done | bytes 1081376 | tf_op jit(solution)/shard_map/ppermute | solution.py:243
  75.9 1.0 fusion.2
  76.9 1.3 slice.74
  78.2 0.5 collective-permute-start.2
  78.8 1.3 slice.75
  80.1 2.9 %collective-permute-start.3 = (bf16[176,3072]{1,0:T(8,128)(2,1)S(1)}, bf16[176,3072]{1,0:T(8,128)(2,1)S(1)}, u32[]{:S(2)}, u32[]{:S(2)}) collective-permute-start(bf16[176,3072]{1,0:T(8,128)(2,1)S(1)} %slice.75), channel_id=1, source_target_pairs={{0,3},{1,0},{2,1},{3,2},{4,7},{5,4},{6,5},{7,6},{8,11},{9,8},{10,9... | collective-permute-start | bytes 3244040 | tf_op jit(solution)/shard_map/ppermute | solution.py:244
  83.0 29.3 %shard_map.77 = (bf16[1408,2304]{1,0:T(8,128)(2,1)}, bf16[176,3072]{1,0:T(8,128)(2,1)S(1)}, bf16[176,3072]{1,0:T(8,128)(2,1)S(1)}, f32[176,3072]{1,0:T(8,128)S(1)}, f32[176,3072]{1,0:T(8,128)}) custom-call(s32[1]{0:T(128)} %bitcast.refs_0_.me, bf16[1408,2304]{1,0:T(8,128)(2,1)} %get-tuple-element.13.refs_1_, ...), custom_call_target="tpu_custom_call", output_to_operand_aliasing={{0}: (1, {})} | custom-call | flops 19931332608 | bytes 28311552 | tf_op jit(solution)/shard_map/pallas_call | solution.py:80
  112.3 0.9 collective-permute-start.7
  113.1 1.2 collective-permute-start.4
  114.4 2.3 fusion.1
  116.7 5.5 %collective-permute-done.2.refs_2_.refs_4_ = bf16[176,3072]{1,0:T(8,128)(2,1)S(1)} collective-permute-done((bf16[176,3072]{1,0:T(8,128)(2,1)S(1)}, bf16[176,3072]{1,0:T(8,128)(2,1)S(1)}, u32[]{:S(2)}, u32[]{:S(2)}) %collective-permute-start.2) | collective-permute-done | bytes 1081376 | tf_op jit(solution)/shard_map/ppermute | solution.py:243
  122.2 1.0 copy-done.8
  123.2 2.0 collective-permute-start.14
  125.2 1.0 copy-done.11
  126.2 1.2 copy-done.9
  127.5 1.2 copy-done.12
  128.7 17.9 %shard_map.78 = (bf16[1408,2304]{1,0:T(8,128)(2,1)}, f32[352,3072]{1,0:T(8,128)S(1)}) custom-call(s32[1]{0:T(128)} %bitcast.refs_0_.me, bf16[1408,2304]{1,0:T(8,128)(2,1)} %get-tuple-element.15.refs_1_, bf16[176,3072]{1,0:T(8,128)(2,1)S(1)} %copy-done.9, bf16[176,3072]{1,0:T(8,128)(2,1)S(1)} %copy-done.12, ...), custom_call_target="tpu_custom_call", output_to_operand_aliasing={{0}: (1, {})} | custom-call | flops 9965666304 | bytes 28311552 | tf_op jit(solution)/shard_map/pallas_call | solution.py:80
  146.6 3.3 %collective-permute-start.19 = (bf16[176,1536]{1,0:T(8,128)(2,1)}, bf16[176,1536]{1,0:T(8,128)(2,1)S(1)}, u32[]{:S(2)}, u32[]{:S(2)}) collective-permute-start(bf16[176,1536]{1,0:T(8,128)(2,1)} %get-tuple-element.25), channel_id=1, source_target_pairs={{0,3},{1,0},{2,1},{3,2},{4,7},{5,4},{6,5},{7,6},{8,11},{9,8},{10,9... | collective-permute-start | bytes 1622024 | tf_op jit(solution)/shard_map/ppermute | solution.py:244
  150.0 1.7 add_convert_fusion
  151.7 0.6 copy-done.10
  152.2 0.3 copy-done.13
  152.6 3.2 %copy-done.3 = bf16[2304,1408]{1,0:T(8,128)(2,1)S(1)} copy-done((bf16[2304,1408]{1,0:T(8,128)(2,1)S(1)}, bf16[2304,1408]{1,0:T(8,128)(2,1)}, u32[]{:S(2)}) %copy-start.3) | copy-done | bytes 6488088
  155.8 27.1 %shard_map.84 = bf16[2304,3072]{1,0:T(8,128)(2,1)} custom-call(s32[1]{0:T(128)} %bitcast.refs_0_.me, bf16[2304,1408]{1,0:T(8,128)(2,1)S(1)} %copy-done.3, bf16[352,3072]{1,0:T(8,128)(2,1)} %collective-permute-done.refs_2_.refs_1_, bf16[352,3072]{1,0:T(8,128)(2,1)} %collective-permute-done.1.refs_3_.refs_2_, bf16[352,3072]{1,0:T(8,128)(2,1)S(1)} %copy-done.5, ...), custom_call_target="tpu_custom_call" | custom-call | flops 19931332608 | bytes 37945344 | tf_op jit(solution)/shard_map/pallas_call | solution.py:182
  182.9 0.1 collective-permute-start.16
  183.1 3.2 %collective-permute-start.17 = (bf16[176,1536]{1,0:T(8,128)(2,1)S(1)}, bf16[176,1536]{1,0:T(8,128)(2,1)S(1)}, u32[]{:S(2)}, u32[]{:S(2)}) collective-permute-start(bf16[176,1536]{1,0:T(8,128)(2,1)S(1)} %copy-done.16), channel_id=1, source_target_pairs={{0,3},{1,0},{2,1},{3,2},{4,7},{5,4},{6,5},{7,6},{8,11},{9,8},{10,9... | collective-permute-start | bytes 1622024 | tf_op jit(solution)/shard_map/ppermute | solution.py:244
  186.3 0.6 collective-permute-start.8
  186.9 15.4 %shard_map.81.refs_8_ = bf16[3072,2304]{1,0:T(8,128)(2,1)} custom-call(bf16[176,3072]{1,0:T(8,128)(2,1)S(1)} %collective-permute-done.12.refs_0_, bf16[176,3072]{1,0:T(8,128)(2,1)} %collective-permute-done.13.refs_1_, bf16[176,3072]{1,0:T(8,128)(2,1)} %collective-permute-done.14.refs_2_, bf16[176,3072]{1,0:T(8,128)(2,1)} %collective-permute-done.15.refs_3_, ...), custom_call_target="tpu_custom_call" | custom-call | flops 9965666304 | bytes 17891328 | tf_op jit(solution)/shard_map/pallas_call | solution.py:222
  202.5 1.5 collective-permute-start.6
  203.9 14.6 %collective-permute-done.8 = bf16[176,3072]{1,0:T(8,128)(2,1)S(1)} collective-permute-done((bf16[176,3072]{1,0:T(8,128)(2,1)S(1)}, bf16[176,3072]{1,0:T(8,128)(2,1)S(1)}, u32[]{:S(2)}, u32[]{:S(2)}) %collective-permute-start.8) | collective-permute-done | bytes 1081376 | tf_op jit(solution)/shard_map/ppermute | solution.py:244
  218.6 3.3 %collective-permute-start.9 = (bf16[32,3072]{1,0:T(8,128)(2,1)S(1)}, bf16[32,3072]{1,0:T(8,128)(2,1)S(1)}, u32[]{:S(2)}, u32[]{:S(2)}) collective-permute-start(bf16[32,3072]{1,0:T(8,128)(2,1)S(1)} %add_convert_fusion.4), channel_id=1, source_target_pairs={{0,3},{1,0},{2,1},{3,2},{4,7},{5,4},{6,5},{7,6},{8,11},{9,8},{10,9... | collective-permute-start | bytes 589832 | tf_op jit(solution)/shard_map/ppermute | solution.py:244
  221.9 0.2 add_convert_fusion.3
  222.2 0.2 add_convert_fusion.2
  222.4 3.3 %collective-permute-start.11 = (bf16[144,3072]{1,0:T(8,128)(2,1)S(1)}, bf16[144,3072]{1,0:T(8,128)(2,1)S(1)}, u32[]{:S(2)}, u32[]{:S(2)}) collective-permute-start(bf16[144,3072]{1,0:T(8,128)(2,1)S(1)} %add_convert_fusion.2), channel_id=1, source_target_pairs={{0,3},{1,0},{2,1},{3,2},{4,7},{5,4},{6,5},{7,6},{8,11},{9,8},{10,9... | collective-permute-start | bytes 2654216 | tf_op jit(solution)/shard_map/ppermute | solution.py:244
  225.7 15.1 %shard_map.82 = bf16[3072,2304]{1,0:T(8,128)(2,1)} custom-call(bf16[176,3072]{1,0:T(8,128)(2,1)S(1)} %collective-permute-done.12.refs_0_, bf16[176,3072]{1,0:T(8,128)(2,1)} %collective-permute-done.13.refs_1_, bf16[176,3072]{1,0:T(8,128)(2,1)} %collective-permute-done.14.refs_2_, ...), custom_call_target="tpu_custom_call", output_to_operand_aliasing={{}: (8, {})} | custom-call | flops 9965666304 | bytes 17891328 | tf_op jit(solution)/shard_map/pallas_call | solution.py:222
  240.8 1.5 collective-permute-done.11.u
  242.3 1.9 shard_map.79._
  244.2 0.8 shard_map.80
  (65 shorter events, 0.3 us)
Async XLA Ops:
  0.6 76.3 %collective-permute-start = (bf16[352,3072]{1,0:T(8,128)(2,1)}, bf16[352,3072]{1,0:T(8,128)(2,1)}, u32[]{:S(2)}, u32[]{:S(2)}) collective-permute-start(bf16[352,3072]{1,0:T(8,128)(2,1)} %refs_3_.3), channel_id=1, source_target_pairs={{0,1},{1,2},{2,3},{3,0},{4,5},{5,6},{6,7},{7,4},{8,9},{9,10},{10,1... | collective-permute-start | bytes 6488072 | tf_op jit(solution)/shard_map/ppermute | solution.py:243
  3.1 75.7 %collective-permute-start.1 = (bf16[352,3072]{1,0:T(8,128)(2,1)}, bf16[352,3072]{1,0:T(8,128)(2,1)}, u32[]{:S(2)}, u32[]{:S(2)}) collective-permute-start(bf16[352,3072]{1,0:T(8,128)(2,1)} %refs_3_.3), channel_id=1, source_target_pairs={{0,3},{1,0},{2,1},{3,2},{4,7},{5,4},{6,5},{7,6},{8,11},{9,8},{10,9... | collective-permute-start | bytes 6488072 | tf_op jit(solution)/shard_map/ppermute | solution.py:244
  4.7 13.8 %slice-start = ((s8[6488064]{0:T(1024)(128)(4,1)}), s8[2293760]{0:T(1024)(128)(4,1)S(1)}, s32[]{:S(2)}) async-start(s8[6488064]{0:T(1024)(128)(4,1)} %bitcast.1), calls=%async_computation | async-start | bytes 4587520
  7.9 68.0 %collective-permute-start.12 = (bf16[176,3072]{1,0:T(8,128)(2,1)}, bf16[176,3072]{1,0:T(8,128)(2,1)S(1)}, u32[]{:S(2)}, u32[]{:S(2)}) collective-permute-start(bf16[176,3072]{1,0:T(8,128)(2,1)} %get-tuple-element.24), channel_id=1, source_target_pairs={{0,1},{1,2},{2,3},{3,0},{4,5},{5,6},{6,7},{7,4},{8,9},{9,10},{10,1... | collective-permute-start | bytes 3244040 | tf_op jit(solution)/shard_map/ppermute | solution.py:243
  8.3 174.7 %collective-permute-start.13 = (bf16[176,3072]{1,0:T(8,128)(2,1)}, bf16[176,3072]{1,0:T(8,128)(2,1)}, u32[]{:S(2)}, u32[]{:S(2)}) collective-permute-start(bf16[176,3072]{1,0:T(8,128)(2,1)} %get-tuple-element.23), channel_id=1, source_target_pairs={{0,1},{1,2},{2,3},{3,0},{4,5},{5,6},{6,7},{7,4},{8,9},{9,10},{10,1... | collective-permute-start | bytes 3244040 | tf_op jit(solution)/shard_map/ppermute | solution.py:243
  9.9 103.2 %collective-permute-start.15 = (bf16[176,3072]{1,0:T(8,128)(2,1)}, bf16[176,3072]{1,0:T(8,128)(2,1)}, u32[]{:S(2)}, u32[]{:S(2)}) collective-permute-start(bf16[176,3072]{1,0:T(8,128)(2,1)} %get-tuple-element.23), channel_id=1, source_target_pairs={{0,3},{1,0},{2,1},{3,2},{4,7},{5,4},{6,5},{7,6},{8,11},{9,8},{10,9... | collective-permute-start | bytes 3244040 | tf_op jit(solution)/shard_map/ppermute | solution.py:244
  11.5 2.8 %copy-start = (bf16[1408,2304]{1,0:T(8,128)(2,1)S(1)}, bf16[1408,2304]{1,0:T(8,128)(2,1)}, u32[]{:S(2)}) copy-start(bf16[1408,2304]{1,0:T(8,128)(2,1)} %pre.1) | copy-start | bytes 19464196
  14.3 4.2 %slice-start.1 = ((s8[6488064]{0:T(1024)(128)(4,1)}), s8[4194304]{0:T(1024)(128)(4,1)S(1)}, s32[]{:S(2)}) async-start(s8[6488064]{0:T(1024)(128)(4,1)} %bitcast.1), calls=%async_computation.1 | async-start | bytes 8388608
  14.3 5.2 %copy-start.4 = (bf16[352,3072]{1,0:T(8,128)(2,1)S(1)}, bf16[352,3072]{1,0:T(8,128)(2,1)}, u32[]{:S(2)}) copy-start(bf16[352,3072]{1,0:T(8,128)(2,1)} %refs_3_.3) | copy-start | bytes 6488068
  37.3 2.0 copy-start.1
  78.2 44.0 %collective-permute-start.2 = (bf16[176,3072]{1,0:T(8,128)(2,1)S(1)}, bf16[176,3072]{1,0:T(8,128)(2,1)S(1)}, u32[]{:S(2)}, u32[]{:S(2)}) collective-permute-start(bf16[176,3072]{1,0:T(8,128)(2,1)S(1)} %slice.74), channel_id=1, source_target_pairs={{0,1},{1,2},{2,3},{3,0},{4,5},{5,6},{6,7},{7,4},{8,9},{9,10},{10,1... | collective-permute-start | bytes 3244040 | tf_op jit(solution)/shard_map/ppermute | solution.py:243
  80.1 45.1 %collective-permute-start.3 = (bf16[176,3072]{1,0:T(8,128)(2,1)S(1)}, bf16[176,3072]{1,0:T(8,128)(2,1)S(1)}, u32[]{:S(2)}, u32[]{:S(2)}) collective-permute-start(bf16[176,3072]{1,0:T(8,128)(2,1)S(1)} %slice.75), channel_id=1, source_target_pairs={{0,3},{1,0},{2,1},{3,2},{4,7},{5,4},{6,5},{7,6},{8,11},{9,8},{10,9... | collective-permute-start | bytes 3244040 | tf_op jit(solution)/shard_map/ppermute | solution.py:244
  82.9 43.3 %slice-start.2 = ((s8[6488064]{0:T(1024)(128)(4,1)}), s8[4194304]{0:T(1024)(128)(4,1)S(1)}, s32[]{:S(2)}) async-start(s8[6488064]{0:T(1024)(128)(4,1)} %bitcast.3), calls=%async_computation.2 | async-start | bytes 8388608
  83.0 43.3 %slice-start.3 = ((s8[6488064]{0:T(1024)(128)(4,1)}), s8[2293760]{0:T(1024)(128)(4,1)S(1)}, s32[]{:S(2)}) async-start(s8[6488064]{0:T(1024)(128)(4,1)} %bitcast.3), calls=%async_computation.3 | async-start | bytes 4587520
  112.3 34.4 %copy-start.6 = (f32[176,3072]{1,0:T(8,128)}, f32[176,3072]{1,0:T(8,128)S(1)}, u32[]{:S(2)}) copy-start(f32[176,3072]{1,0:T(8,128)S(1)} %get-tuple-element.14) | copy-start | bytes 6488068
  112.3 34.4 %collective-permute-start.7 = (bf16[176,3072]{1,0:T(8,128)(2,1)S(1)}, bf16[176,3072]{1,0:T(8,128)(2,1)S(1)}, u32[]{:S(2)}, u32[]{:S(2)}) collective-permute-start(bf16[176,3072]{1,0:T(8,128)(2,1)S(1)} %get-tuple-element.19), channel_id=1, source_target_pairs={{0,3},{1,0},{2,1},{3,2},{4,7},{5,4},{6,5},{7,6},{8,11},{9,8},{10,9... | collective-permute-start | bytes 3244040 | tf_op jit(solution)/shard_map/ppermute | solution.py:244
  113.1 36.8 %collective-permute-start.4 = (bf16[176,3072]{1,0:T(8,128)(2,1)S(1)}, bf16[176,3072]{1,0:T(8,128)(2,1)S(1)}, u32[]{:S(2)}, u32[]{:S(2)}) collective-permute-start(bf16[176,3072]{1,0:T(8,128)(2,1)S(1)} %get-tuple-element.17), channel_id=1, source_target_pairs={{0,1},{1,2},{2,3},{3,0},{4,5},{5,6},{6,7},{7,4},{8,9},{9,10},{10,1... | collective-permute-start | bytes 3244040 | tf_op jit(solution)/shard_map/ppermute | solution.py:243
  122.2 1.0 copy-start.8
  123.2 59.8 %collective-permute-start.14 = (bf16[176,3072]{1,0:T(8,128)(2,1)}, bf16[176,3072]{1,0:T(8,128)(2,1)}, u32[]{:S(2)}, u32[]{:S(2)}) collective-permute-start(bf16[176,3072]{1,0:T(8,128)(2,1)} %get-tuple-element.24), channel_id=1, source_target_pairs={{0,3},{1,0},{2,1},{3,2},{4,7},{5,4},{6,5},{7,6},{8,11},{9,8},{10,9... | collective-permute-start | bytes 3244040 | tf_op jit(solution)/shard_map/ppermute | solution.py:244
  125.2 1.0 copy-start.11
  126.2 60.0 %collective-permute-start.18 = (bf16[176,1536]{1,0:T(8,128)(2,1)}, bf16[176,1536]{1,0:T(8,128)(2,1)}, u32[]{:S(2)}, u32[]{:S(2)}) collective-permute-start(bf16[176,1536]{1,0:T(8,128)(2,1)} %get-tuple-element.27), channel_id=1, source_target_pairs={{0,1},{1,2},{2,3},{3,0},{4,5},{5,6},{6,7},{7,4},{8,9},{9,10},{10,1... | collective-permute-start | bytes 1622024 | tf_op jit(solution)/shard_map/ppermute | solution.py:243
  126.2 1.2 copy-start.9
  127.5 1.2 copy-start.12
  146.6 40.2 %collective-permute-start.19 = (bf16[176,1536]{1,0:T(8,128)(2,1)}, bf16[176,1536]{1,0:T(8,128)(2,1)S(1)}, u32[]{:S(2)}, u32[]{:S(2)}) collective-permute-start(bf16[176,1536]{1,0:T(8,128)(2,1)} %get-tuple-element.25), channel_id=1, source_target_pairs={{0,3},{1,0},{2,1},{3,2},{4,7},{5,4},{6,5},{7,6},{8,11},{9,8},{10,9... | collective-permute-start | bytes 1622024 | tf_op jit(solution)/shard_map/ppermute | solution.py:244
  149.9 1.7 copy-start.5
  149.9 2.3 copy-start.10
  150.0 2.6 %copy-start.13 = (bf16[176,3072]{1,0:T(8,128)(2,1)S(1)}, bf16[176,3072]{1,0:T(8,128)(2,1)}, u32[]{:S(2)}) copy-start(bf16[176,3072]{1,0:T(8,128)(2,1)} %copy-done.11) | copy-start | bytes 3244036
  151.6 35.3 %slice-start.4 = ((s8[6488064]{0:T(1024)(128)(4,1)}), s8[4194304]{0:T(1024)(128)(4,1)S(1)}, s32[]{:S(2)}) async-start(s8[6488064]{0:T(1024)(128)(4,1)} %bitcast.5), calls=%async_computation.4 | async-start | bytes 8388608
  151.6 35.3 %slice-start.5 = ((s8[6488064]{0:T(1024)(128)(4,1)}), s8[2293760]{0:T(1024)(128)(4,1)S(1)}, s32[]{:S(2)}) async-start(s8[6488064]{0:T(1024)(128)(4,1)} %bitcast.5), calls=%async_computation.5 | async-start | bytes 4587520
  151.6 35.3 %copy-start.2 = (bf16[352,3072]{1,0:T(8,128)(2,1)S(1)}, bf16[352,3072]{1,0:T(8,128)(2,1)}, u32[]{:S(2)}) copy-start(bf16[352,3072]{1,0:T(8,128)(2,1)} %refs_4_.9) | copy-start | bytes 6488068
  151.6 50.8 %collective-permute-start.5 = (bf16[176,3072]{1,0:T(8,128)(2,1)}, bf16[176,3072]{1,0:T(8,128)(2,1)S(1)}, u32[]{:S(2)}, u32[]{:S(2)}) collective-permute-start(bf16[176,3072]{1,0:T(8,128)(2,1)} %get-tuple-element.22), channel_id=1, source_target_pairs={{0,1},{1,2},{2,3},{3,0},{4,5},{5,6},{6,7},{7,4},{8,9},{9,10},{10,1... | collective-permute-start | bytes 3244040 | tf_op jit(solution)/shard_map/ppermute | solution.py:243
  152.6 3.2 %copy-start.3 = (bf16[2304,1408]{1,0:T(8,128)(2,1)S(1)}, bf16[2304,1408]{1,0:T(8,128)(2,1)}, u32[]{:S(2)}) copy-start(bf16[2304,1408]{1,0:T(8,128)(2,1)} %shard_map.83.refs_0_) | copy-start | bytes 19464196
  155.8 27.1 %copy-start.15 = (bf16[176,1536]{1,0:T(8,128)(2,1)S(1)}, bf16[176,1536]{1,0:T(8,128)(2,1)}, u32[]{:S(2)}) copy-start(bf16[176,1536]{1,0:T(8,128)(2,1)} %get-tuple-element.28) | copy-start | bytes 1622020
  155.8 27.2 %copy-start.16 = (bf16[176,1536]{1,0:T(8,128)(2,1)S(1)}, bf16[176,1536]{1,0:T(8,128)(2,1)}, u32[]{:S(2)}) copy-start(bf16[176,1536]{1,0:T(8,128)(2,1)} %get-tuple-element.26) | copy-start | bytes 1622020
  182.9 39.5 %collective-permute-start.16 = (bf16[176,1536]{1,0:T(8,128)(2,1)S(1)}, bf16[176,1536]{1,0:T(8,128)(2,1)S(1)}, u32[]{:S(2)}, u32[]{:S(2)}) collective-permute-start(bf16[176,1536]{1,0:T(8,128)(2,1)S(1)} %copy-done.15), channel_id=1, source_target_pairs={{0,1},{1,2},{2,3},{3,0},{4,5},{5,6},{6,7},{7,4},{8,9},{9,10},{10,1... | collective-permute-start | bytes 1622024 | tf_op jit(solution)/shard_map/ppermute | solution.py:243
  183.1 42.7 %collective-permute-start.17 = (bf16[176,1536]{1,0:T(8,128)(2,1)S(1)}, bf16[176,1536]{1,0:T(8,128)(2,1)S(1)}, u32[]{:S(2)}, u32[]{:S(2)}) collective-permute-start(bf16[176,1536]{1,0:T(8,128)(2,1)S(1)} %copy-done.16), channel_id=1, source_target_pairs={{0,3},{1,0},{2,1},{3,2},{4,7},{5,4},{6,5},{7,6},{8,11},{9,8},{10,9... | collective-permute-start | bytes 1622024 | tf_op jit(solution)/shard_map/ppermute | solution.py:244
  186.3 32.3 %collective-permute-start.8 = (bf16[176,3072]{1,0:T(8,128)(2,1)S(1)}, bf16[176,3072]{1,0:T(8,128)(2,1)S(1)}, u32[]{:S(2)}, u32[]{:S(2)}) collective-permute-start(bf16[176,3072]{1,0:T(8,128)(2,1)S(1)} %get-tuple-element.21), channel_id=1, source_target_pairs={{0,3},{1,0},{2,1},{3,2},{4,7},{5,4},{6,5},{7,6},{8,11},{9,8},{10,9... | collective-permute-start | bytes 3244040 | tf_op jit(solution)/shard_map/ppermute | solution.py:244
  186.9 15.5 %copy-start.7 = (f32[176,3072]{1,0:T(8,128)S(1)}, f32[176,3072]{1,0:T(8,128)}, u32[]{:S(2)}) copy-start(f32[176,3072]{1,0:T(8,128)} %copy-done.6) | copy-start | bytes 6488068
  186.9 31.6 %copy-start.14 = (f32[176,3072]{1,0:T(8,128)S(1)}, f32[176,3072]{1,0:T(8,128)}, u32[]{:S(2)}) copy-start(f32[176,3072]{1,0:T(8,128)} %get-tuple-element.18) | copy-start | bytes 6488068
  202.5 41.7 %collective-permute-start.6 = (bf16[32,3072]{1,0:T(8,128)(2,1)S(1)}, bf16[32,3072]{1,0:T(8,128)(2,1)S(1)}, u32[]{:S(2)}, u32[]{:S(2)}) collective-permute-start(bf16[32,3072]{1,0:T(8,128)(2,1)S(1)} %add_convert_fusion.5), channel_id=1, source_target_pairs={{0,1},{1,2},{2,3},{3,0},{4,5},{5,6},{6,7},{7,4},{8,9},{9,10},{10,1... | collective-permute-start | bytes 589832 | tf_op jit(solution)/shard_map/ppermute | solution.py:243
  218.6 25.6 %collective-permute-start.9 = (bf16[32,3072]{1,0:T(8,128)(2,1)S(1)}, bf16[32,3072]{1,0:T(8,128)(2,1)S(1)}, u32[]{:S(2)}, u32[]{:S(2)}) collective-permute-start(bf16[32,3072]{1,0:T(8,128)(2,1)S(1)} %add_convert_fusion.4), channel_id=1, source_target_pairs={{0,3},{1,0},{2,1},{3,2},{4,7},{5,4},{6,5},{7,6},{8,11},{9,8},{10,9... | collective-permute-start | bytes 589832 | tf_op jit(solution)/shard_map/ppermute | solution.py:244
  222.1 18.7 %collective-permute-start.10 = (bf16[144,3072]{1,0:T(8,128)(2,1)S(1)}, bf16[144,3072]{1,0:T(8,128)(2,1)S(1)}, u32[]{:S(2)}, u32[]{:S(2)}) collective-permute-start(bf16[144,3072]{1,0:T(8,128)(2,1)S(1)} %add_convert_fusion.3), channel_id=1, source_target_pairs={{0,1},{1,2},{2,3},{3,0},{4,5},{5,6},{6,7},{7,4},{8,9},{9,10},{10,1... | collective-permute-start | bytes 2654216 | tf_op jit(solution)/shard_map/ppermute | solution.py:243
  222.2 20.1 %slice-start.6 = ((s8[4325376]{0:T(1024)(128)(4,1)}), s8[4194304]{0:T(1024)(128)(4,1)S(1)}, s32[]{:S(2)}) async-start(s8[4325376]{0:T(1024)(128)(4,1)} %bitcast.7), calls=%async_computation.6 | async-start | bytes 8388608
  222.4 19.9 %slice-start.7 = ((s8[4325376]{0:T(1024)(128)(4,1)}), s8[131072]{0:T(1024)(128)(4,1)S(1)}, s32[]{:S(2)}) async-start(s8[4325376]{0:T(1024)(128)(4,1)} %bitcast.7), calls=%async_computation.7 | async-start | bytes 262144
  222.4 19.8 %collective-permute-start.11 = (bf16[144,3072]{1,0:T(8,128)(2,1)S(1)}, bf16[144,3072]{1,0:T(8,128)(2,1)S(1)}, u32[]{:S(2)}, u32[]{:S(2)}) collective-permute-start(bf16[144,3072]{1,0:T(8,128)(2,1)S(1)} %add_convert_fusion.2), channel_id=1, source_target_pairs={{0,3},{1,0},{2,1},{3,2},{4,7},{5,4},{6,5},{7,6},{8,11},{9,8},{10,9... | collective-permute-start | bytes 2654216 | tf_op jit(solution)/shard_map/ppermute | solution.py:244

commit v2 on v1

--- a/solution.py
+++ b/solution.py
@@ -11,7 +11,7 @@
 TN = (((0,), (0,)), ((), ()))
 F32, BF16 = jnp.float32, jnp.bfloat16
 TILE = 768
-LAST = 32
+LAST = 24
 MIB = 2**20
 
 
@@ -150,7 +150,7 @@
         in_specs=[pl.BlockSpec((rows, TILE), lambda i: (0, i))],
         out_specs=pl.BlockSpec((TILE, rows), lambda i: (i, 0)),
         out_shape=pltpu.HBM((ff, rows), BF16),
-        compiler_params=pltpu.CompilerParams(vmem_limit_bytes=24 * MIB, dimension_semantics=("arbitrary",)),
+        compiler_params=pltpu.CompilerParams(vmem_limit_bytes=58 * MIB, dimension_semantics=("arbitrary",)),
         cost_estimate=pl.CostEstimate(flops=4 * rows * ff, bytes_accessed=4 * rows * ff, transcendentals=0),
     )(pre)
 
@@ -190,7 +190,7 @@
             scratch_shapes=[pltpu.VMEM((rows, tn), BF16)],
         ),
         out_shape=jax.ShapeDtypeStruct((ff, d), BF16),
-        compiler_params=pltpu.CompilerParams(vmem_limit_bytes=32 * MIB, dimension_semantics=("arbitrary", "arbitrary")),
+        compiler_params=pltpu.CompilerParams(vmem_limit_bytes=58 * MIB, dimension_semantics=("arbitrary", "arbitrary")),
         cost_estimate=pl.CostEstimate(flops=2 * rows * ff * d, bytes_accessed=2 * (rows * ff + 2 * rows * d + ff * d), transcendentals=0),
     )(me, hidden, *dys)
 

time: 246 us -> 242 us (0.984)
  waiting for transfers between devices: 58.2 us -> 51.8 us
  Pallas kernels: 130 us -> 135 us
  local copies, waits for them, and re-layouts: 23.6 us -> 19.9 us
    unnamed x50 -> x18, local copies, waits for them, and re-layouts: 14.5 us -> 8.92 us
    ppermute x10, waiting for transfers between devices: 16.1 us -> 11.5 us  [send(): b = lax.ppermute(b, 'tp', left)]
    pallas_call x1, Pallas kernels: 4.21 us -> 7.41 us  [hidden_transposed(): pl.pallas_call(hidden_body, grid=(ff // TILE,), in_specs=[pl.BlockSpec((r...]
  transfers between devices with their start and end apart: 20 -> 20, of which waited for: 4 -> 5; matrix products, arithmetic and copies ran while one was open for 5% -> 6% of each run, Pallas kernels for 53% -> 55%
where the time goes in v2:
time: 242 us; the launch traced here: 241 us
  Pallas kernels  135 us (56%)
  waiting for transfers between devices  51.8 us (21%)
  starting transfers between devices  29.9 us (12%)
  local copies, waits for them, and re-layouts  19.9 us (8%)
  other arithmetic  4.55 us (2%)
    pallas_call x3, Pallas kernels, backward(): pl.pallas_call(functools.partial(backward_body, nd, len(dys), blocks, len...  65.6 us
    ppermute x10, waiting for transfers between devices, send(): a = lax.ppermute(a, 'tp', right)  40.3 us
    pallas_call x2, Pallas kernels, grad_w_in(): pl.pallas_call(functools.partial(dw_in_body, columns), grid=(ff // tn,),...  30.6 us
    pallas_call x1, Pallas kernels, grad_w_down(): pl.pallas_call(body, grid_spec=pltpu.PrefetchScalarGridSpec(num_scalar_pr...  28.2 us
    ppermute x10, starting transfers between devices, send(): b = lax.ppermute(b, 'tp', left)  22.1 us
    ppermute x10, waiting for transfers between devices, send(): b = lax.ppermute(b, 'tp', left)  11.5 us
    unnamed x18, local copies, waits for them, and re-layouts  8.92 us
    ppermute x10, starting transfers between devices, send(): a = lax.ppermute(a, 'tp', right)  7.71 us
  transfers between devices with their start and end apart: 20, of which 5 were waited for; matrix products, arithmetic and copies ran while one was open for 6% of the time, Pallas kernels for 55%

profile of v2, /device:TPU:112, one launch (start us, length us, event | category | flops | bytes accessed | tf_op | source)
XLA Modules:
  0.0 241.5 jit_solution(13282262784293485573)
XLA Ops:
  0.6 2.4 %collective-permute-start = (bf16[352,3072]{1,0:T(8,128)(2,1)}, bf16[352,3072]{1,0:T(8,128)(2,1)}, u32[]{:S(2)}, u32[]{:S(2)}) collective-permute-start(bf16[352,3072]{1,0:T(8,128)(2,1)} %refs_3_.3), channel_id=1, source_target_pairs={{0,1},{1,2},{2,3},{3,0},{4,5},{5,6},{6,7},{7,4},{8,9},{9,10},{10,1... | collective-permute-start | bytes 6488072 | tf_op jit(solution)/shard_map/ppermute | solution.py:243
  3.1 1.6 collective-permute-start.1
  4.7 3.0 %fusion = (bf16[176,3072]{1,0:T(8,128)(2,1)}, bf16[176,3072]{1,0:T(8,128)(2,1)}) fusion(bf16[352,3072]{1,0:T(8,128)(2,1)} %refs_4_.9), kind=kLoop, calls=%fused_computation.6 | loop fusion | bytes 4325376 | tf_op jit(solution)/shard_map/slice | solution.py:263
  7.7 0.4 collective-permute-start.12
  8.1 1.6 collective-permute-start.13
  9.7 1.6 collective-permute-start.15
  11.3 7.4 %shard_map.83.refs_0_ = bf16[2304,1408]{1,0:T(8,128)(2,1)} custom-call(bf16[1408,2304]{1,0:T(8,128)(2,1)} %pre.1), custom_call_target="tpu_custom_call" | custom-call | flops 12976128 | bytes 12976128 | tf_op jit(solution)/shard_map/pallas_call | solution.py:147
  18.7 2.8 %copy-done = bf16[1408,2304]{1,0:T(8,128)(2,1)S(1)} copy-done((bf16[1408,2304]{1,0:T(8,128)(2,1)S(1)}, bf16[1408,2304]{1,0:T(8,128)(2,1)}, u32[]{:S(2)}) %copy-start) | copy-done | bytes 6488088
  21.6 1.6 copy-done.3
  23.2 17.8 %shard_map.76 = (bf16[1408,2304]{1,0:T(8,128)(2,1)}, f32[352,3072]{1,0:T(8,128)S(1)}) custom-call(s32[1]{0:T(128)} %bitcast.refs_0_.me, bf16[352,3072]{1,0:T(8,128)(2,1)S(1)} %copy-done.3, bf16[1408,2304]{1,0:T(8,128)(2,1)S(1)} %copy-done, bf16[2304,3072]{1,0:T(8,128)(2,1)} %refs_5_.3, bf16[3072,2304]{1,0:T(8,128)(2,1)} %refs_6_.3), custom_call_target="tpu_custom_call" | custom-call | flops 9965666304 | bytes 28311552 | tf_op jit(solution)/shard_map/pallas_call | solution.py:80
  41.0 34.9 %collective-permute-done.12.refs_0_ = bf16[176,3072]{1,0:T(8,128)(2,1)S(1)} collective-permute-done((bf16[176,3072]{1,0:T(8,128)(2,1)}, bf16[176,3072]{1,0:T(8,128)(2,1)S(1)}, u32[]{:S(2)}, u32[]{:S(2)}) %collective-permute-start.12) | collective-permute-done | bytes 1081376 | tf_op jit(solution)/shard_map/ppermute | solution.py:243
  75.9 1.1 fusion.2
  77.0 2.3 slice.74
  79.3 0.5 collective-permute-start.2
  79.7 0.0 collective-permute-done.1.refs_3_.refs_2_
  79.7 2.3 slice.75
  82.0 2.8 %collective-permute-start.3 = (bf16[176,3072]{1,0:T(8,128)(2,1)}, bf16[176,3072]{1,0:T(8,128)(2,1)}, u32[]{:S(2)}, u32[]{:S(2)}) collective-permute-start(bf16[176,3072]{1,0:T(8,128)(2,1)} %slice.75), channel_id=1, source_target_pairs={{0,3},{1,0},{2,1},{3,2},{4,7},{5,4},{6,5},{7,6},{8,11},{9,8},{10,9... | collective-permute-start | bytes 3244040 | tf_op jit(solution)/shard_map/ppermute | solution.py:244
  84.8 29.3 %shard_map.77 = (bf16[1408,2304]{1,0:T(8,128)(2,1)}, bf16[176,3072]{1,0:T(8,128)(2,1)S(1)}, bf16[176,3072]{1,0:T(8,128)(2,1)S(1)}, f32[176,3072]{1,0:T(8,128)S(1)}, f32[176,3072]{1,0:T(8,128)}) custom-call(s32[1]{0:T(128)} %bitcast.refs_0_.me, bf16[1408,2304]{1,0:T(8,128)(2,1)} %get-tuple-element.13.refs_1_, ...), custom_call_target="tpu_custom_call", output_to_operand_aliasing={{0}: (1, {})} | custom-call | flops 19931332608 | bytes 28311552 | tf_op jit(solution)/shard_map/pallas_call | solution.py:80
  114.1 0.9 collective-permute-start.7
  115.0 0.0 collective-permute-done.15.refs_3_
  115.0 1.2 collective-permute-start.4
  116.2 2.3 fusion.1
  118.5 3.8 %collective-permute-done.2.refs_2_.refs_4_ = bf16[176,3072]{1,0:T(8,128)(2,1)} collective-permute-done((bf16[176,3072]{1,0:T(8,128)(2,1)}, bf16[176,3072]{1,0:T(8,128)(2,1)}, u32[]{:S(2)}, u32[]{:S(2)}) %collective-permute-start.2) | collective-permute-done | bytes 1081376 | tf_op jit(solution)/shard_map/ppermute | solution.py:243
  122.3 2.0 collective-permute-start.14
  124.3 0.0 collective-permute-start.18
  124.4 18.5 %shard_map.78 = (bf16[1408,2304]{1,0:T(8,128)(2,1)}, f32[352,3072]{1,0:T(8,128)S(1)}) custom-call(s32[1]{0:T(128)} %bitcast.refs_0_.me, bf16[1408,2304]{1,0:T(8,128)(2,1)} %get-tuple-element.15.refs_1_, bf16[176,3072]{1,0:T(8,128)(2,1)} %collective-permute-done.2.refs_2_.refs_4_, ...), custom_call_target="tpu_custom_call", output_to_operand_aliasing={{0}: (1, {})} | custom-call | flops 9965666304 | bytes 28311552 | tf_op jit(solution)/shard_map/pallas_call | solution.py:80
  142.9 3.3 %collective-permute-start.19 = (bf16[176,1536]{1,0:T(8,128)(2,1)}, bf16[176,1536]{1,0:T(8,128)(2,1)}, u32[]{:S(2)}, u32[]{:S(2)}) collective-permute-start(bf16[176,1536]{1,0:T(8,128)(2,1)} %get-tuple-element.25), channel_id=1, source_target_pairs={{0,3},{1,0},{2,1},{3,2},{4,7},{5,4},{6,5},{7,6},{8,11},{9,8},{10,9... | collective-permute-start | bytes 1622024 | tf_op jit(solution)/shard_map/ppermute | solution.py:244
  146.2 2.0 add_convert_fusion
  148.2 28.2 %shard_map.84 = bf16[2304,3072]{1,0:T(8,128)(2,1)} custom-call(s32[1]{0:T(128)} %bitcast.refs_0_.me, bf16[2304,1408]{1,0:T(8,128)(2,1)} %shard_map.83.refs_0_, bf16[352,3072]{1,0:T(8,128)(2,1)} %collective-permute-done.refs_2_.refs_1_, bf16[352,3072]{1,0:T(8,128)(2,1)} %collective-permute-done.1.refs_3_.refs_2_, bf16[352,3072]{1,0:T(8,128)(2,1)} %refs_3_.3, ...), custom_call_target="tpu_custom_call" | custom-call | flops 19931332608 | bytes 37945344 | tf_op jit(solution)/shard_map/pallas_call | solution.py:182
  176.4 1.2 collective-permute-start.16
  177.6 2.1 collective-permute-start.17
  179.7 1.8 collective-permute-start.8
  181.5 2.8 %copy-done.1 = bf16[1408,2304]{1,0:T(8,128)(2,1)S(1)} copy-done((bf16[1408,2304]{1,0:T(8,128)(2,1)S(1)}, bf16[1408,2304]{1,0:T(8,128)(2,1)}, u32[]{:S(2)}) %copy-start.1) | copy-done | bytes 6488088
  184.4 1.6 copy-done.2
  186.0 15.6 %shard_map.81.refs_8_ = bf16[3072,2304]{1,0:T(8,128)(2,1)} custom-call(bf16[176,3072]{1,0:T(8,128)(2,1)S(1)} %collective-permute-done.12.refs_0_, bf16[176,3072]{1,0:T(8,128)(2,1)} %collective-permute-done.13.refs_1_, bf16[176,3072]{1,0:T(8,128)(2,1)} %collective-permute-done.14.refs_2_, bf16[176,3072]{1,0:T(8,128)(2,1)} %collective-permute-done.15.refs_3_, ...), custom_call_target="tpu_custom_call" | custom-call | flops 9965666304 | bytes 17891328 | tf_op jit(solution)/shard_map/pallas_call | solution.py:222
  201.6 0.9 add_convert_fusion.5
  202.5 0.3 collective-permute-start.6
  202.8 10.5 %collective-permute-done.8 = bf16[176,3072]{1,0:T(8,128)(2,1)S(1)} collective-permute-done((bf16[176,3072]{1,0:T(8,128)(2,1)}, bf16[176,3072]{1,0:T(8,128)(2,1)S(1)}, u32[]{:S(2)}, u32[]{:S(2)}) %collective-permute-start.8) | collective-permute-done | bytes 1081376 | tf_op jit(solution)/shard_map/ppermute | solution.py:244
  213.3 2.8 %collective-permute-start.9 = (bf16[24,3072]{1,0:T(8,128)(2,1)S(1)}, bf16[24,3072]{1,0:T(8,128)(2,1)S(1)}, u32[]{:S(2)}, u32[]{:S(2)}) collective-permute-start(bf16[24,3072]{1,0:T(8,128)(2,1)S(1)} %add_convert_fusion.4), channel_id=1, source_target_pairs={{0,3},{1,0},{2,1},{3,2},{4,7},{5,4},{6,5},{7,6},{8,11},{9,8},{10,9... | collective-permute-start | bytes 442376 | tf_op jit(solution)/shard_map/ppermute | solution.py:244
  216.1 1.4 add_convert_fusion.3
  217.5 0.1 collective-permute-start.10
  217.6 0.2 add_convert_fusion.2
  217.8 3.3 %collective-permute-start.11 = (bf16[152,3072]{1,0:T(8,128)(2,1)S(1)}, bf16[152,3072]{1,0:T(8,128)(2,1)S(1)}, u32[]{:S(2)}, u32[]{:S(2)}) collective-permute-start(bf16[152,3072]{1,0:T(8,128)(2,1)S(1)} %add_convert_fusion.2), channel_id=1, source_target_pairs={{0,3},{1,0},{2,1},{3,2},{4,7},{5,4},{6,5},{7,6},{8,11},{9,8},{10,9... | collective-permute-start | bytes 2801672 | tf_op jit(solution)/shard_map/ppermute | solution.py:244
  221.1 15.1 %shard_map.82 = bf16[3072,2304]{1,0:T(8,128)(2,1)} custom-call(bf16[176,3072]{1,0:T(8,128)(2,1)S(1)} %collective-permute-done.12.refs_0_, bf16[176,3072]{1,0:T(8,128)(2,1)} %collective-permute-done.13.refs_1_, bf16[176,3072]{1,0:T(8,128)(2,1)} %collective-permute-done.14.refs_2_, ...), custom_call_target="tpu_custom_call", output_to_operand_aliasing={{}: (8, {})} | custom-call | flops 9965666304 | bytes 17891328 | tf_op jit(solution)/shard_map/pallas_call | solution.py:222
  236.2 1.6 collective-permute-done.10.s
  237.7 1.0 collective-permute-done.11.u
  238.8 1.9 shard_map.79._
  240.7 0.8 shard_map.80
  (30 shorter events, 0.1 us)
Async XLA Ops:
  0.6 76.3 %collective-permute-start = (bf16[352,3072]{1,0:T(8,128)(2,1)}, bf16[352,3072]{1,0:T(8,128)(2,1)}, u32[]{:S(2)}, u32[]{:S(2)}) collective-permute-start(bf16[352,3072]{1,0:T(8,128)(2,1)} %refs_3_.3), channel_id=1, source_target_pairs={{0,1},{1,2},{2,3},{3,0},{4,5},{5,6},{6,7},{7,4},{8,9},{9,10},{10,1... | collective-permute-start | bytes 6488072 | tf_op jit(solution)/shard_map/ppermute | solution.py:243
  3.1 76.7 %collective-permute-start.1 = (bf16[352,3072]{1,0:T(8,128)(2,1)}, bf16[352,3072]{1,0:T(8,128)(2,1)}, u32[]{:S(2)}, u32[]{:S(2)}) collective-permute-start(bf16[352,3072]{1,0:T(8,128)(2,1)} %refs_3_.3), channel_id=1, source_target_pairs={{0,3},{1,0},{2,1},{3,2},{4,7},{5,4},{6,5},{7,6},{8,11},{9,8},{10,9... | collective-permute-start | bytes 6488072 | tf_op jit(solution)/shard_map/ppermute | solution.py:244
  7.7 68.2 %collective-permute-start.12 = (bf16[176,3072]{1,0:T(8,128)(2,1)}, bf16[176,3072]{1,0:T(8,128)(2,1)S(1)}, u32[]{:S(2)}, u32[]{:S(2)}) collective-permute-start(bf16[176,3072]{1,0:T(8,128)(2,1)} %get-tuple-element.24), channel_id=1, source_target_pairs={{0,1},{1,2},{2,3},{3,0},{4,5},{5,6},{6,7},{7,4},{8,9},{9,10},{10,1... | collective-permute-start | bytes 3244040 | tf_op jit(solution)/shard_map/ppermute | solution.py:243
  8.1 168.3 %collective-permute-start.13 = (bf16[176,3072]{1,0:T(8,128)(2,1)}, bf16[176,3072]{1,0:T(8,128)(2,1)}, u32[]{:S(2)}, u32[]{:S(2)}) collective-permute-start(bf16[176,3072]{1,0:T(8,128)(2,1)} %get-tuple-element.23), channel_id=1, source_target_pairs={{0,1},{1,2},{2,3},{3,0},{4,5},{5,6},{6,7},{7,4},{8,9},{9,10},{10,1... | collective-permute-start | bytes 3244040 | tf_op jit(solution)/shard_map/ppermute | solution.py:243
  9.7 105.2 %collective-permute-start.15 = (bf16[176,3072]{1,0:T(8,128)(2,1)}, bf16[176,3072]{1,0:T(8,128)(2,1)}, u32[]{:S(2)}, u32[]{:S(2)}) collective-permute-start(bf16[176,3072]{1,0:T(8,128)(2,1)} %get-tuple-element.23), channel_id=1, source_target_pairs={{0,3},{1,0},{2,1},{3,2},{4,7},{5,4},{6,5},{7,6},{8,11},{9,8},{10,9... | collective-permute-start | bytes 3244040 | tf_op jit(solution)/shard_map/ppermute | solution.py:244
  18.7 2.8 %copy-start = (bf16[1408,2304]{1,0:T(8,128)(2,1)S(1)}, bf16[1408,2304]{1,0:T(8,128)(2,1)}, u32[]{:S(2)}) copy-start(bf16[1408,2304]{1,0:T(8,128)(2,1)} %pre.1) | copy-start | bytes 19464196
  21.6 1.6 copy-start.3
  79.3 43.1 %collective-permute-start.2 = (bf16[176,3072]{1,0:T(8,128)(2,1)}, bf16[176,3072]{1,0:T(8,128)(2,1)}, u32[]{:S(2)}, u32[]{:S(2)}) collective-permute-start(bf16[176,3072]{1,0:T(8,128)(2,1)} %slice.74), channel_id=1, source_target_pairs={{0,1},{1,2},{2,3},{3,0},{4,5},{5,6},{6,7},{7,4},{8,9},{9,10},{10,1... | collective-permute-start | bytes 3244040 | tf_op jit(solution)/shard_map/ppermute | solution.py:243
  82.0 42.3 %collective-permute-start.3 = (bf16[176,3072]{1,0:T(8,128)(2,1)}, bf16[176,3072]{1,0:T(8,128)(2,1)}, u32[]{:S(2)}, u32[]{:S(2)}) collective-permute-start(bf16[176,3072]{1,0:T(8,128)(2,1)} %slice.75), channel_id=1, source_target_pairs={{0,3},{1,0},{2,1},{3,2},{4,7},{5,4},{6,5},{7,6},{8,11},{9,8},{10,9... | collective-permute-start | bytes 3244040 | tf_op jit(solution)/shard_map/ppermute | solution.py:244
  84.8 39.6 %slice-start = ((s8[6488064]{0:T(1024)(128)(4,1)}), s8[4194304]{0:T(1024)(128)(4,1)S(1)}, s32[]{:S(2)}) async-start(s8[6488064]{0:T(1024)(128)(4,1)} %bitcast.1), calls=%async_computation | async-start | bytes 8388608
  84.8 39.6 %slice-start.1 = ((s8[6488064]{0:T(1024)(128)(4,1)}), s8[2293760]{0:T(1024)(128)(4,1)S(1)}, s32[]{:S(2)}) async-start(s8[6488064]{0:T(1024)(128)(4,1)} %bitcast.1), calls=%async_computation.1 | async-start | bytes 4587520
  114.1 28.8 %copy-start.4 = (f32[176,3072]{1,0:T(8,128)}, f32[176,3072]{1,0:T(8,128)S(1)}, u32[]{:S(2)}) copy-start(f32[176,3072]{1,0:T(8,128)S(1)} %get-tuple-element.14) | copy-start | bytes 6488068
  114.1 28.8 %collective-permute-start.7 = (bf16[176,3072]{1,0:T(8,128)(2,1)S(1)}, bf16[176,3072]{1,0:T(8,128)(2,1)S(1)}, u32[]{:S(2)}, u32[]{:S(2)}) collective-permute-start(bf16[176,3072]{1,0:T(8,128)(2,1)S(1)} %get-tuple-element.19), channel_id=1, source_target_pairs={{0,3},{1,0},{2,1},{3,2},{4,7},{5,4},{6,5},{7,6},{8,11},{9,8},{10,9... | collective-permute-start | bytes 3244040 | tf_op jit(solution)/shard_map/ppermute | solution.py:244
  115.0 31.2 %collective-permute-start.4 = (bf16[176,3072]{1,0:T(8,128)(2,1)S(1)}, bf16[176,3072]{1,0:T(8,128)(2,1)S(1)}, u32[]{:S(2)}, u32[]{:S(2)}) collective-permute-start(bf16[176,3072]{1,0:T(8,128)(2,1)S(1)} %get-tuple-element.17), channel_id=1, source_target_pairs={{0,1},{1,2},{2,3},{3,0},{4,5},{5,6},{6,7},{7,4},{8,9},{9,10},{10,1... | collective-permute-start | bytes 3244040 | tf_op jit(solution)/shard_map/ppermute | solution.py:243
  122.3 55.2 %collective-permute-start.14 = (bf16[176,3072]{1,0:T(8,128)(2,1)}, bf16[176,3072]{1,0:T(8,128)(2,1)}, u32[]{:S(2)}, u32[]{:S(2)}) collective-permute-start(bf16[176,3072]{1,0:T(8,128)(2,1)} %get-tuple-element.24), channel_id=1, source_target_pairs={{0,3},{1,0},{2,1},{3,2},{4,7},{5,4},{6,5},{7,6},{8,11},{9,8},{10,9... | collective-permute-start | bytes 3244040 | tf_op jit(solution)/shard_map/ppermute | solution.py:244
  124.3 55.4 %collective-permute-start.18 = (bf16[176,1536]{1,0:T(8,128)(2,1)}, bf16[176,1536]{1,0:T(8,128)(2,1)}, u32[]{:S(2)}, u32[]{:S(2)}) collective-permute-start(bf16[176,1536]{1,0:T(8,128)(2,1)} %get-tuple-element.27), channel_id=1, source_target_pairs={{0,1},{1,2},{2,3},{3,0},{4,5},{5,6},{6,7},{7,4},{8,9},{9,10},{10,1... | collective-permute-start | bytes 1622024 | tf_op jit(solution)/shard_map/ppermute | solution.py:243
  142.9 38.6 %collective-permute-start.19 = (bf16[176,1536]{1,0:T(8,128)(2,1)}, bf16[176,1536]{1,0:T(8,128)(2,1)}, u32[]{:S(2)}, u32[]{:S(2)}) collective-permute-start(bf16[176,1536]{1,0:T(8,128)(2,1)} %get-tuple-element.25), channel_id=1, source_target_pairs={{0,3},{1,0},{2,1},{3,2},{4,7},{5,4},{6,5},{7,6},{8,11},{9,8},{10,9... | collective-permute-start | bytes 1622024 | tf_op jit(solution)/shard_map/ppermute | solution.py:244
  148.2 53.4 %collective-permute-start.5 = (bf16[176,3072]{1,0:T(8,128)(2,1)}, bf16[176,3072]{1,0:T(8,128)(2,1)}, u32[]{:S(2)}, u32[]{:S(2)}) collective-permute-start(bf16[176,3072]{1,0:T(8,128)(2,1)} %get-tuple-element.22), channel_id=1, source_target_pairs={{0,1},{1,2},{2,3},{3,0},{4,5},{5,6},{6,7},{7,4},{8,9},{9,10},{10,1... | collective-permute-start | bytes 3244040 | tf_op jit(solution)/shard_map/ppermute | solution.py:243
  176.4 41.4 %collective-permute-start.16 = (bf16[176,1536]{1,0:T(8,128)(2,1)}, bf16[176,1536]{1,0:T(8,128)(2,1)S(1)}, u32[]{:S(2)}, u32[]{:S(2)}) collective-permute-start(bf16[176,1536]{1,0:T(8,128)(2,1)} %get-tuple-element.28), channel_id=1, source_target_pairs={{0,1},{1,2},{2,3},{3,0},{4,5},{5,6},{6,7},{7,4},{8,9},{9,10},{10,1... | collective-permute-start | bytes 1622024 | tf_op jit(solution)/shard_map/ppermute | solution.py:243
  177.6 43.5 %collective-permute-start.17 = (bf16[176,1536]{1,0:T(8,128)(2,1)}, bf16[176,1536]{1,0:T(8,128)(2,1)S(1)}, u32[]{:S(2)}, u32[]{:S(2)}) collective-permute-start(bf16[176,1536]{1,0:T(8,128)(2,1)} %get-tuple-element.26), channel_id=1, source_target_pairs={{0,3},{1,0},{2,1},{3,2},{4,7},{5,4},{6,5},{7,6},{8,11},{9,8},{10,9... | collective-permute-start | bytes 1622024 | tf_op jit(solution)/shard_map/ppermute | solution.py:244
  179.7 33.6 %collective-permute-start.8 = (bf16[176,3072]{1,0:T(8,128)(2,1)}, bf16[176,3072]{1,0:T(8,128)(2,1)S(1)}, u32[]{:S(2)}, u32[]{:S(2)}) collective-permute-start(bf16[176,3072]{1,0:T(8,128)(2,1)} %get-tuple-element.21), channel_id=1, source_target_pairs={{0,3},{1,0},{2,1},{3,2},{4,7},{5,4},{6,5},{7,6},{8,11},{9,8},{10,9... | collective-permute-start | bytes 3244040 | tf_op jit(solution)/shard_map/ppermute | solution.py:244
  181.5 2.8 %copy-start.1 = (bf16[1408,2304]{1,0:T(8,128)(2,1)S(1)}, bf16[1408,2304]{1,0:T(8,128)(2,1)}, u32[]{:S(2)}) copy-start(bf16[1408,2304]{1,0:T(8,128)(2,1)} %get-tuple-element.20.refs_7_) | copy-start | bytes 19464196
  184.4 1.6 copy-start.2
  186.0 15.6 %copy-start.5 = (f32[176,3072]{1,0:T(8,128)S(1)}, f32[176,3072]{1,0:T(8,128)}, u32[]{:S(2)}) copy-start(f32[176,3072]{1,0:T(8,128)} %copy-done.4) | copy-start | bytes 6488068
  186.0 27.3 %copy-start.6 = (f32[176,3072]{1,0:T(8,128)S(1)}, f32[176,3072]{1,0:T(8,128)}, u32[]{:S(2)}) copy-start(f32[176,3072]{1,0:T(8,128)} %get-tuple-element.18) | copy-start | bytes 6488068
  202.5 38.1 %collective-permute-start.6 = (bf16[24,3072]{1,0:T(8,128)(2,1)S(1)}, bf16[24,3072]{1,0:T(8,128)(2,1)S(1)}, u32[]{:S(2)}, u32[]{:S(2)}) collective-permute-start(bf16[24,3072]{1,0:T(8,128)(2,1)S(1)} %add_convert_fusion.5), channel_id=1, source_target_pairs={{0,1},{1,2},{2,3},{3,0},{4,5},{5,6},{6,7},{7,4},{8,9},{9,10},{10,1... | collective-permute-start | bytes 442376 | tf_op jit(solution)/shard_map/ppermute | solution.py:243
  213.3 27.4 %collective-permute-start.9 = (bf16[24,3072]{1,0:T(8,128)(2,1)S(1)}, bf16[24,3072]{1,0:T(8,128)(2,1)S(1)}, u32[]{:S(2)}, u32[]{:S(2)}) collective-permute-start(bf16[24,3072]{1,0:T(8,128)(2,1)S(1)} %add_convert_fusion.4), channel_id=1, source_target_pairs={{0,3},{1,0},{2,1},{3,2},{4,7},{5,4},{6,5},{7,6},{8,11},{9,8},{10,9... | collective-permute-start | bytes 442376 | tf_op jit(solution)/shard_map/ppermute | solution.py:244
  217.5 20.2 %collective-permute-start.10 = (bf16[152,3072]{1,0:T(8,128)(2,1)S(1)}, bf16[152,3072]{1,0:T(8,128)(2,1)S(1)}, u32[]{:S(2)}, u32[]{:S(2)}) collective-permute-start(bf16[152,3072]{1,0:T(8,128)(2,1)S(1)} %add_convert_fusion.3), channel_id=1, source_target_pairs={{0,1},{1,2},{2,3},{3,0},{4,5},{5,6},{6,7},{7,4},{8,9},{9,10},{10,1... | collective-permute-start | bytes 2801672 | tf_op jit(solution)/shard_map/ppermute | solution.py:243
  217.8 21.0 %collective-permute-start.11 = (bf16[152,3072]{1,0:T(8,128)(2,1)S(1)}, bf16[152,3072]{1,0:T(8,128)(2,1)S(1)}, u32[]{:S(2)}, u32[]{:S(2)}) collective-permute-start(bf16[152,3072]{1,0:T(8,128)(2,1)S(1)} %add_convert_fusion.2), channel_id=1, source_target_pairs={{0,3},{1,0},{2,1},{3,2},{4,7},{5,4},{6,5},{7,6},{8,11},{9,8},{10,9... | collective-permute-start | bytes 2801672 | tf_op jit(solution)/shard_map/ppermute | solution.py:244

commit v3 on v2

--- a/solution.py
+++ b/solution.py
@@ -92,7 +92,7 @@
         ),
         out_shape=[pltpu.HBM((pre.shape[0], ff), BF16)] + [jax.ShapeDtypeStruct((r, d), t) for r, t in terms],
         input_output_aliases={1: 0} if chained else {},
-        compiler_params=pltpu.CompilerParams(vmem_limit_bytes=(36 if blocks == 1 else 48) * MIB, dimension_semantics=("arbitrary",)),
+        compiler_params=pltpu.CompilerParams(vmem_limit_bytes=(32 if blocks == 1 else 44) * MIB, dimension_semantics=("arbitrary",)),
         cost_estimate=pl.CostEstimate(flops=4 * total * d * ff, bytes_accessed=4 * d * ff, transcendentals=0),
     )(me, *chained, *dys, *[pre] * blocks, w_down, w_in)
 
@@ -114,7 +114,7 @@
     tn = d // 2
     middle = 2 * s1.shape[0]
     spec = lambda r: pl.BlockSpec((r, tn), lambda j: (0, j))
-    params = pltpu.CompilerParams(vmem_limit_bytes=16 * MIB, dimension_semantics=("arbitrary",))
+    params = pltpu.CompilerParams(vmem_limit_bytes=10 * MIB, dimension_semantics=("arbitrary",))
     dx = pl.pallas_call(
         most_body,
         grid=(d // tn,),
@@ -150,7 +150,7 @@
         in_specs=[pl.BlockSpec((rows, TILE), lambda i: (0, i))],
         out_specs=pl.BlockSpec((TILE, rows), lambda i: (i, 0)),
         out_shape=pltpu.HBM((ff, rows), BF16),
-        compiler_params=pltpu.CompilerParams(vmem_limit_bytes=58 * MIB, dimension_semantics=("arbitrary",)),
+        compiler_params=pltpu.CompilerParams(vmem_limit_bytes=20 * MIB, dimension_semantics=("arbitrary",)),
         cost_estimate=pl.CostEstimate(flops=4 * rows * ff, bytes_accessed=4 * rows * ff, transcendentals=0),
     )(pre)
 
@@ -190,7 +190,7 @@
             scratch_shapes=[pltpu.VMEM((rows, tn), BF16)],
         ),
         out_shape=jax.ShapeDtypeStruct((ff, d), BF16),
-        compiler_params=pltpu.CompilerParams(vmem_limit_bytes=58 * MIB, dimension_semantics=("arbitrary", "arbitrary")),
+        compiler_params=pltpu.CompilerParams(vmem_limit_bytes=28 * MIB, dimension_semantics=("arbitrary", "arbitrary")),
         cost_estimate=pl.CostEstimate(flops=2 * rows * ff * d, bytes_accessed=2 * (rows * ff + 2 * rows * d + ff * d), transcendentals=0),
     )(me, hidden, *dys)
 
@@ -229,7 +229,7 @@
         scratch_shapes=[pltpu.VMEM((rows, m), BF16), pltpu.SemaphoreType.DMA((len(xs),))],
         out_shape=jax.ShapeDtypeStruct((d, ff), BF16),
         input_output_aliases={len(xs) + 1: 0} if chained else {},
-        compiler_params=pltpu.CompilerParams(vmem_limit_bytes=26 * MIB, dimension_semantics=("arbitrary",)),
+        compiler_params=pltpu.CompilerParams(vmem_limit_bytes=22 * MIB, dimension_semantics=("arbitrary",)),
         cost_estimate=pl.CostEstimate(flops=2 * rows * m * ff, bytes_accessed=2 * (rows * m + rows * ff + m * ff), transcendentals=0),
     )(*xs, d_pre, *chained)
 

time: 242 us -> 246 us (1.017)
  waiting for transfers between devices: 51.8 us -> 58.9 us
  Pallas kernels: 135 us -> 129 us
  local copies, waits for them, and re-layouts: 19.9 us -> 24.5 us
  other arithmetic: 4.55 us -> 1.16 us
    unnamed x18 -> x52, local copies, waits for them, and re-layouts: 8.92 us -> 15.3 us
    ppermute x10, waiting for transfers between devices: 11.5 us -> 15.8 us  [send(): b = lax.ppermute(b, 'tp', left)]
    convert_element_type x5, other arithmetic: 4.55 us -> 1.16 us  [add(): return (term + got.astype(F32)).astype(BF16)]
    pallas_call x1, Pallas kernels: 7.41 us -> 4.21 us  [hidden_transposed(): pl.pallas_call(hidden_body, grid=(ff // TILE,), in_specs=[pl.BlockSpec((r...]
    ppermute x10, waiting for transfers between devices: 40.3 us -> 43 us  [send(): a = lax.ppermute(a, 'tp', right)]
  transfers between devices with their start and end apart: 20 -> 20, of which waited for: 5 -> 5; matrix products, arithmetic and copies ran while one was open for 6% -> 4% of each run, Pallas kernels for 55% -> 52%
where the time goes in v3:
time: 246 us; the launch traced here: 245 us
  Pallas kernels  129 us (52%)
  waiting for transfers between devices  58.9 us (24%)
  starting transfers between devices  30.6 us (12%)
  local copies, waits for them, and re-layouts  24.5 us (10%)
    pallas_call x3, Pallas kernels, backward(): pl.pallas_call(functools.partial(backward_body, nd, len(dys), blocks, len...  64.9 us
    ppermute x10, waiting for transfers between devices, send(): a = lax.ppermute(a, 'tp', right)  43 us
    pallas_call x2, Pallas kernels, grad_w_in(): pl.pallas_call(functools.partial(dw_in_body, columns), grid=(ff // tn,),...  30.5 us
    pallas_call x1, Pallas kernels, grad_w_down(): pl.pallas_call(body, grid_spec=pltpu.PrefetchScalarGridSpec(num_scalar_pr...  27 us
    ppermute x10, starting transfers between devices, send(): b = lax.ppermute(b, 'tp', left)  22.1 us
    ppermute x10, waiting for transfers between devices, send(): b = lax.ppermute(b, 'tp', left)  15.8 us
    unnamed x52, local copies, waits for them, and re-layouts  15.3 us
    ppermute x10, starting transfers between devices, send(): a = lax.ppermute(a, 'tp', right)  8.51 us
  transfers between devices with their start and end apart: 20, of which 5 were waited for; matrix products, arithmetic and copies ran while one was open for 4% of the time, Pallas kernels for 52%

profile of v3, /device:TPU:112, one launch (start us, length us, event | category | flops | bytes accessed | tf_op | source)
XLA Modules:
  0.0 245.4 jit_solution(2690302824084374468)
XLA Ops:
  0.6 2.4 collective-permute-start
  3.1 1.6 collective-permute-start.1
  4.7 3.2 %fusion = (bf16[176,3072]{1,0:T(8,128)(2,1)}, bf16[176,3072]{1,0:T(8,128)(2,1)}) fusion(bf16[352,3072]{1,0:T(8,128)(2,1)} %refs_4_.9), kind=kLoop, calls=%fused_computation.6 | loop fusion | bytes 4325376 | tf_op jit(solution)/shard_map/slice | solution.py:263
  7.9 0.4 collective-permute-start.12
  8.3 1.6 collective-permute-start.13
  9.9 1.6 collective-permute-start.15
  11.5 2.8 %copy-done = bf16[1408,2304]{1,0:T(8,128)(2,1)S(1)} copy-done((bf16[1408,2304]{1,0:T(8,128)(2,1)S(1)}, bf16[1408,2304]{1,0:T(8,128)(2,1)}, u32[]{:S(2)}) %copy-start) | copy-done | bytes 6488088
  14.3 4.2 %shard_map.83.refs_0_ = bf16[2304,1408]{1,0:T(8,128)(2,1)} custom-call(bf16[1408,2304]{1,0:T(8,128)(2,1)S(1)} %copy-done), custom_call_target="tpu_custom_call" | custom-call | flops 12976128 | bytes 12976128 | tf_op jit(solution)/shard_map/pallas_call | solution.py:147
  18.6 0.9 copy-done.4
  19.5 17.8 %shard_map.76 = (bf16[1408,2304]{1,0:T(8,128)(2,1)}, f32[352,3072]{1,0:T(8,128)S(1)}) custom-call(s32[1]{0:T(128)} %bitcast.refs_0_.me, bf16[352,3072]{1,0:T(8,128)(2,1)S(1)} %copy-done.4, bf16[1408,2304]{1,0:T(8,128)(2,1)S(1)} %bitcast.2, bf16[2304,3072]{1,0:T(8,128)(2,1)} %refs_5_.3, bf16[3072,2304]{1,0:T(8,128)(2,1)} %refs_6_.3), custom_call_target="tpu_custom_call" | custom-call | flops 9965666304 | bytes 28311552 | tf_op jit(solution)/shard_map/pallas_call | solution.py:80
  37.3 2.0 copy-done.1
  39.3 36.6 %collective-permute-done.12.refs_0_ = bf16[176,3072]{1,0:T(8,128)(2,1)S(1)} collective-permute-done((bf16[176,3072]{1,0:T(8,128)(2,1)}, bf16[176,3072]{1,0:T(8,128)(2,1)S(1)}, u32[]{:S(2)}, u32[]{:S(2)}) %collective-permute-start.12) | collective-permute-done | bytes 1081376 | tf_op jit(solution)/shard_map/ppermute | solution.py:243
  75.9 1.1 fusion.2
  77.0 1.3 slice.74
  78.3 0.5 collective-permute-start.2
  78.8 1.3 slice.75
  80.1 2.9 %collective-permute-start.3 = (bf16[176,3072]{1,0:T(8,128)(2,1)S(1)}, bf16[176,3072]{1,0:T(8,128)(2,1)S(1)}, u32[]{:S(2)}, u32[]{:S(2)}) collective-permute-start(bf16[176,3072]{1,0:T(8,128)(2,1)S(1)} %slice.75), channel_id=1, source_target_pairs={{0,3},{1,0},{2,1},{3,2},{4,7},{5,4},{6,5},{7,6},{8,11},{9,8},{10,9... | collective-permute-start | bytes 3244040 | tf_op jit(solution)/shard_map/ppermute | solution.py:244
  83.0 29.2 %shard_map.77 = (bf16[1408,2304]{1,0:T(8,128)(2,1)}, bf16[176,3072]{1,0:T(8,128)(2,1)S(1)}, bf16[176,3072]{1,0:T(8,128)(2,1)S(1)}, f32[176,3072]{1,0:T(8,128)S(1)}, f32[176,3072]{1,0:T(8,128)S(1)}) custom-call(s32[1]{0:T(128)} %bitcast.refs_0_.me, bf16[1408,2304]{1,0:T(8,128)(2,1)} %get-tuple-element.13.refs_1_, ...), custom_call_target="tpu_custom_call", output_to_operand_aliasing={{0}: (1, {})} | custom-call | flops 19931332608 | bytes 28311552 | tf_op jit(solution)/shard_map/pallas_call | solution.py:80
  112.2 0.9 collective-permute-start.7
  113.1 1.2 collective-permute-start.4
  114.3 2.3 fusion.1
  116.6 5.6 %collective-permute-done.2.refs_2_.refs_4_ = bf16[176,3072]{1,0:T(8,128)(2,1)S(1)} collective-permute-done((bf16[176,3072]{1,0:T(8,128)(2,1)S(1)}, bf16[176,3072]{1,0:T(8,128)(2,1)S(1)}, u32[]{:S(2)}, u32[]{:S(2)}) %collective-permute-start.2) | collective-permute-done | bytes 1081376 | tf_op jit(solution)/shard_map/ppermute | solution.py:243
  122.2 1.0 copy-done.10
  123.2 2.0 collective-permute-start.14
  125.2 1.0 copy-done.13
  126.2 1.2 copy-done.11
  127.5 1.2 copy-done.14
  128.7 17.9 %shard_map.78 = (bf16[1408,2304]{1,0:T(8,128)(2,1)}, f32[352,3072]{1,0:T(8,128)S(1)}) custom-call(s32[1]{0:T(128)} %bitcast.refs_0_.me, bf16[1408,2304]{1,0:T(8,128)(2,1)} %get-tuple-element.15.refs_1_, bf16[176,3072]{1,0:T(8,128)(2,1)S(1)} %copy-done.11, bf16[176,3072]{1,0:T(8,128)(2,1)S(1)} %copy-done.14, ...), custom_call_target="tpu_custom_call", output_to_operand_aliasing={{0}: (1, {})} | custom-call | flops 9965666304 | bytes 28311552 | tf_op jit(solution)/shard_map/pallas_call | solution.py:80
  146.7 3.3 %collective-permute-start.19 = (bf16[176,1536]{1,0:T(8,128)(2,1)}, bf16[176,1536]{1,0:T(8,128)(2,1)S(1)}, u32[]{:S(2)}, u32[]{:S(2)}) collective-permute-start(bf16[176,1536]{1,0:T(8,128)(2,1)} %get-tuple-element.25), channel_id=1, source_target_pairs={{0,3},{1,0},{2,1},{3,2},{4,7},{5,4},{6,5},{7,6},{8,11},{9,8},{10,9... | collective-permute-start | bytes 1622024 | tf_op jit(solution)/shard_map/ppermute | solution.py:244
  150.0 0.7 add_convert_fusion
  150.8 0.8 copy-done.5
  151.6 0.3 copy-done.12
  151.8 0.3 copy-done.15
  152.2 3.6 %copy-done.3 = bf16[2304,1408]{1,0:T(8,128)(2,1)S(1)} copy-done((bf16[2304,1408]{1,0:T(8,128)(2,1)S(1)}, bf16[2304,1408]{1,0:T(8,128)(2,1)}, u32[]{:S(2)}) %copy-start.3) | copy-done | bytes 6488088
  155.8 27.0 %shard_map.84 = bf16[2304,3072]{1,0:T(8,128)(2,1)} custom-call(s32[1]{0:T(128)} %bitcast.refs_0_.me, bf16[2304,1408]{1,0:T(8,128)(2,1)S(1)} %copy-done.3, bf16[352,3072]{1,0:T(8,128)(2,1)} %collective-permute-done.refs_2_.refs_1_, bf16[352,3072]{1,0:T(8,128)(2,1)} %collective-permute-done.1.refs_3_.refs_2_, bf16[352,3072]{1,0:T(8,128)(2,1)S(1)} %copy-done.5, ...), custom_call_target="tpu_custom_call" | custom-call | flops 19931332608 | bytes 37945344 | tf_op jit(solution)/shard_map/pallas_call | solution.py:182
  183.0 3.2 %collective-permute-start.17 = (bf16[176,1536]{1,0:T(8,128)(2,1)S(1)}, bf16[176,1536]{1,0:T(8,128)(2,1)S(1)}, u32[]{:S(2)}, u32[]{:S(2)}) collective-permute-start(bf16[176,1536]{1,0:T(8,128)(2,1)S(1)} %copy-done.17), channel_id=1, source_target_pairs={{0,3},{1,0},{2,1},{3,2},{4,7},{5,4},{6,5},{7,6},{8,11},{9,8},{10,9... | collective-permute-start | bytes 1622024 | tf_op jit(solution)/shard_map/ppermute | solution.py:244
  186.3 15.4 %shard_map.81.refs_8_ = bf16[3072,2304]{1,0:T(8,128)(2,1)} custom-call(bf16[176,3072]{1,0:T(8,128)(2,1)S(1)} %collective-permute-done.12.refs_0_, bf16[176,3072]{1,0:T(8,128)(2,1)} %collective-permute-done.13.refs_1_, bf16[176,3072]{1,0:T(8,128)(2,1)} %collective-permute-done.14.refs_2_, bf16[176,3072]{1,0:T(8,128)(2,1)} %collective-permute-done.15.refs_3_, ...), custom_call_target="tpu_custom_call" | custom-call | flops 9965666304 | bytes 17891328 | tf_op jit(solution)/shard_map/pallas_call | solution.py:222
  201.8 2.0 collective-permute-start.6
  203.8 14.6 %collective-permute-done.8 = bf16[176,3072]{1,0:T(8,128)(2,1)S(1)} collective-permute-done((bf16[176,3072]{1,0:T(8,128)(2,1)S(1)}, bf16[176,3072]{1,0:T(8,128)(2,1)S(1)}, u32[]{:S(2)}, u32[]{:S(2)}) %collective-permute-start.8) | collective-permute-done | bytes 1081376 | tf_op jit(solution)/shard_map/ppermute | solution.py:244
  218.5 3.3 %collective-permute-start.9 = (bf16[24,3072]{1,0:T(8,128)(2,1)S(1)}, bf16[24,3072]{1,0:T(8,128)(2,1)S(1)}, u32[]{:S(2)}, u32[]{:S(2)}) collective-permute-start(bf16[24,3072]{1,0:T(8,128)(2,1)S(1)} %add_convert_fusion.4), channel_id=1, source_target_pairs={{0,3},{1,0},{2,1},{3,2},{4,7},{5,4},{6,5},{7,6},{8,11},{9,8},{10,9... | collective-permute-start | bytes 442376 | tf_op jit(solution)/shard_map/ppermute | solution.py:244
  221.8 0.2 add_convert_fusion.3
  222.1 0.2 add_convert_fusion.2
  222.3 3.3 %collective-permute-start.11 = (bf16[152,3072]{1,0:T(8,128)(2,1)S(1)}, bf16[152,3072]{1,0:T(8,128)(2,1)S(1)}, u32[]{:S(2)}, u32[]{:S(2)}) collective-permute-start(bf16[152,3072]{1,0:T(8,128)(2,1)S(1)} %add_convert_fusion.2), channel_id=1, source_target_pairs={{0,3},{1,0},{2,1},{3,2},{4,7},{5,4},{6,5},{7,6},{8,11},{9,8},{10,9... | collective-permute-start | bytes 2801672 | tf_op jit(solution)/shard_map/ppermute | solution.py:244
  225.6 15.1 %shard_map.82 = bf16[3072,2304]{1,0:T(8,128)(2,1)} custom-call(bf16[176,3072]{1,0:T(8,128)(2,1)S(1)} %collective-permute-done.12.refs_0_, bf16[176,3072]{1,0:T(8,128)(2,1)} %collective-permute-done.13.refs_1_, bf16[176,3072]{1,0:T(8,128)(2,1)} %collective-permute-done.14.refs_2_, ...), custom_call_target="tpu_custom_call", output_to_operand_aliasing={{}: (8, {})} | custom-call | flops 9965666304 | bytes 17891328 | tf_op jit(solution)/shard_map/pallas_call | solution.py:222
  240.7 0.8 collective-permute-done.10.s
  241.5 1.2 collective-permute-done.11.u
  242.7 1.9 shard_map.79._
  244.6 0.8 shard_map.80
  (67 shorter events, 0.6 us)
Async XLA Ops:
  0.6 76.3 %collective-permute-start = (bf16[352,3072]{1,0:T(8,128)(2,1)}, bf16[352,3072]{1,0:T(8,128)(2,1)}, u32[]{:S(2)}, u32[]{:S(2)}) collective-permute-start(bf16[352,3072]{1,0:T(8,128)(2,1)} %refs_3_.3), channel_id=1, source_target_pairs={{0,1},{1,2},{2,3},{3,0},{4,5},{5,6},{6,7},{7,4},{8,9},{9,10},{10,1... | collective-permute-start | bytes 6488072 | tf_op jit(solution)/shard_map/ppermute | solution.py:243
  3.1 75.8 %collective-permute-start.1 = (bf16[352,3072]{1,0:T(8,128)(2,1)}, bf16[352,3072]{1,0:T(8,128)(2,1)}, u32[]{:S(2)}, u32[]{:S(2)}) collective-permute-start(bf16[352,3072]{1,0:T(8,128)(2,1)} %refs_3_.3), channel_id=1, source_target_pairs={{0,3},{1,0},{2,1},{3,2},{4,7},{5,4},{6,5},{7,6},{8,11},{9,8},{10,9... | collective-permute-start | bytes 6488072 | tf_op jit(solution)/shard_map/ppermute | solution.py:244
  4.7 13.8 %slice-start = ((s8[6488064]{0:T(1024)(128)(4,1)}), s8[2293760]{0:T(1024)(128)(4,1)S(1)}, s32[]{:S(2)}) async-start(s8[6488064]{0:T(1024)(128)(4,1)} %bitcast.1), calls=%async_computation | async-start | bytes 4587520
  7.9 68.0 %collective-permute-start.12 = (bf16[176,3072]{1,0:T(8,128)(2,1)}, bf16[176,3072]{1,0:T(8,128)(2,1)S(1)}, u32[]{:S(2)}, u32[]{:S(2)}) collective-permute-start(bf16[176,3072]{1,0:T(8,128)(2,1)} %get-tuple-element.24), channel_id=1, source_target_pairs={{0,1},{1,2},{2,3},{3,0},{4,5},{5,6},{6,7},{7,4},{8,9},{9,10},{10,1... | collective-permute-start | bytes 3244040 | tf_op jit(solution)/shard_map/ppermute | solution.py:243
  8.3 174.6 %collective-permute-start.13 = (bf16[176,3072]{1,0:T(8,128)(2,1)}, bf16[176,3072]{1,0:T(8,128)(2,1)}, u32[]{:S(2)}, u32[]{:S(2)}) collective-permute-start(bf16[176,3072]{1,0:T(8,128)(2,1)} %get-tuple-element.23), channel_id=1, source_target_pairs={{0,1},{1,2},{2,3},{3,0},{4,5},{5,6},{6,7},{7,4},{8,9},{9,10},{10,1... | collective-permute-start | bytes 3244040 | tf_op jit(solution)/shard_map/ppermute | solution.py:243
  9.9 103.2 %collective-permute-start.15 = (bf16[176,3072]{1,0:T(8,128)(2,1)}, bf16[176,3072]{1,0:T(8,128)(2,1)}, u32[]{:S(2)}, u32[]{:S(2)}) collective-permute-start(bf16[176,3072]{1,0:T(8,128)(2,1)} %get-tuple-element.23), channel_id=1, source_target_pairs={{0,3},{1,0},{2,1},{3,2},{4,7},{5,4},{6,5},{7,6},{8,11},{9,8},{10,9... | collective-permute-start | bytes 3244040 | tf_op jit(solution)/shard_map/ppermute | solution.py:244
  11.5 2.8 %copy-start = (bf16[1408,2304]{1,0:T(8,128)(2,1)S(1)}, bf16[1408,2304]{1,0:T(8,128)(2,1)}, u32[]{:S(2)}) copy-start(bf16[1408,2304]{1,0:T(8,128)(2,1)} %pre.1) | copy-start | bytes 19464196
  14.3 4.2 %slice-start.1 = ((s8[6488064]{0:T(1024)(128)(4,1)}), s8[4194304]{0:T(1024)(128)(4,1)S(1)}, s32[]{:S(2)}) async-start(s8[6488064]{0:T(1024)(128)(4,1)} %bitcast.1), calls=%async_computation.1 | async-start | bytes 8388608
  14.3 5.2 %copy-start.4 = (bf16[352,3072]{1,0:T(8,128)(2,1)S(1)}, bf16[352,3072]{1,0:T(8,128)(2,1)}, u32[]{:S(2)}) copy-start(bf16[352,3072]{1,0:T(8,128)(2,1)} %refs_3_.3) | copy-start | bytes 6488068
  37.3 2.0 copy-start.1
  78.3 43.9 %collective-permute-start.2 = (bf16[176,3072]{1,0:T(8,128)(2,1)S(1)}, bf16[176,3072]{1,0:T(8,128)(2,1)S(1)}, u32[]{:S(2)}, u32[]{:S(2)}) collective-permute-start(bf16[176,3072]{1,0:T(8,128)(2,1)S(1)} %slice.74), channel_id=1, source_target_pairs={{0,1},{1,2},{2,3},{3,0},{4,5},{5,6},{6,7},{7,4},{8,9},{9,10},{10,1... | collective-permute-start | bytes 3244040 | tf_op jit(solution)/shard_map/ppermute | solution.py:243
  80.1 45.1 %collective-permute-start.3 = (bf16[176,3072]{1,0:T(8,128)(2,1)S(1)}, bf16[176,3072]{1,0:T(8,128)(2,1)S(1)}, u32[]{:S(2)}, u32[]{:S(2)}) collective-permute-start(bf16[176,3072]{1,0:T(8,128)(2,1)S(1)} %slice.75), channel_id=1, source_target_pairs={{0,3},{1,0},{2,1},{3,2},{4,7},{5,4},{6,5},{7,6},{8,11},{9,8},{10,9... | collective-permute-start | bytes 3244040 | tf_op jit(solution)/shard_map/ppermute | solution.py:244
  83.0 43.3 %slice-start.2 = ((s8[6488064]{0:T(1024)(128)(4,1)}), s8[4194304]{0:T(1024)(128)(4,1)S(1)}, s32[]{:S(2)}) async-start(s8[6488064]{0:T(1024)(128)(4,1)} %bitcast.3), calls=%async_computation.2 | async-start | bytes 8388608
  83.0 43.3 %slice-start.3 = ((s8[6488064]{0:T(1024)(128)(4,1)}), s8[2293760]{0:T(1024)(128)(4,1)S(1)}, s32[]{:S(2)}) async-start(s8[6488064]{0:T(1024)(128)(4,1)} %bitcast.3), calls=%async_computation.3 | async-start | bytes 4587520
  112.2 34.5 %copy-start.6 = (f32[176,3072]{1,0:T(8,128)}, f32[176,3072]{1,0:T(8,128)S(1)}, u32[]{:S(2)}) copy-start(f32[176,3072]{1,0:T(8,128)S(1)} %get-tuple-element.18) | copy-start | bytes 6488068
  112.2 34.5 %copy-start.8 = (f32[176,3072]{1,0:T(8,128)}, f32[176,3072]{1,0:T(8,128)S(1)}, u32[]{:S(2)}) copy-start(f32[176,3072]{1,0:T(8,128)S(1)} %get-tuple-element.14) | copy-start | bytes 6488068
  112.2 34.5 %collective-permute-start.7 = (bf16[176,3072]{1,0:T(8,128)(2,1)S(1)}, bf16[176,3072]{1,0:T(8,128)(2,1)S(1)}, u32[]{:S(2)}, u32[]{:S(2)}) collective-permute-start(bf16[176,3072]{1,0:T(8,128)(2,1)S(1)} %get-tuple-element.19), channel_id=1, source_target_pairs={{0,3},{1,0},{2,1},{3,2},{4,7},{5,4},{6,5},{7,6},{8,11},{9,8},{10,9... | collective-permute-start | bytes 3244040 | tf_op jit(solution)/shard_map/ppermute | solution.py:244
  113.1 36.9 %collective-permute-start.4 = (bf16[176,3072]{1,0:T(8,128)(2,1)S(1)}, bf16[176,3072]{1,0:T(8,128)(2,1)S(1)}, u32[]{:S(2)}, u32[]{:S(2)}) collective-permute-start(bf16[176,3072]{1,0:T(8,128)(2,1)S(1)} %get-tuple-element.17), channel_id=1, source_target_pairs={{0,1},{1,2},{2,3},{3,0},{4,5},{5,6},{6,7},{7,4},{8,9},{9,10},{10,1... | collective-permute-start | bytes 3244040 | tf_op jit(solution)/shard_map/ppermute | solution.py:243
  122.2 1.0 copy-start.10
  123.2 59.7 %collective-permute-start.14 = (bf16[176,3072]{1,0:T(8,128)(2,1)}, bf16[176,3072]{1,0:T(8,128)(2,1)}, u32[]{:S(2)}, u32[]{:S(2)}) collective-permute-start(bf16[176,3072]{1,0:T(8,128)(2,1)} %get-tuple-element.24), channel_id=1, source_target_pairs={{0,3},{1,0},{2,1},{3,2},{4,7},{5,4},{6,5},{7,6},{8,11},{9,8},{10,9... | collective-permute-start | bytes 3244040 | tf_op jit(solution)/shard_map/ppermute | solution.py:244
  125.2 1.0 copy-start.13
  126.2 59.9 %collective-permute-start.18 = (bf16[176,1536]{1,0:T(8,128)(2,1)}, bf16[176,1536]{1,0:T(8,128)(2,1)}, u32[]{:S(2)}, u32[]{:S(2)}) collective-permute-start(bf16[176,1536]{1,0:T(8,128)(2,1)} %get-tuple-element.27), channel_id=1, source_target_pairs={{0,1},{1,2},{2,3},{3,0},{4,5},{5,6},{6,7},{7,4},{8,9},{9,10},{10,1... | collective-permute-start | bytes 1622024 | tf_op jit(solution)/shard_map/ppermute | solution.py:243
  126.2 1.2 copy-start.11
  127.5 1.2 copy-start.14
  146.7 39.6 %collective-permute-start.19 = (bf16[176,1536]{1,0:T(8,128)(2,1)}, bf16[176,1536]{1,0:T(8,128)(2,1)S(1)}, u32[]{:S(2)}, u32[]{:S(2)}) collective-permute-start(bf16[176,1536]{1,0:T(8,128)(2,1)} %get-tuple-element.25), channel_id=1, source_target_pairs={{0,3},{1,0},{2,1},{3,2},{4,7},{5,4},{6,5},{7,6},{8,11},{9,8},{10,9... | collective-permute-start | bytes 1622024 | tf_op jit(solution)/shard_map/ppermute | solution.py:244
  150.0 1.6 copy-start.5
  150.0 1.9 copy-start.12
  150.0 2.2 copy-start.15
  150.6 35.6 %slice-start.4 = ((s8[6488064]{0:T(1024)(128)(4,1)}), s8[4194304]{0:T(1024)(128)(4,1)S(1)}, s32[]{:S(2)}) async-start(s8[6488064]{0:T(1024)(128)(4,1)} %bitcast.5), calls=%async_computation.4 | async-start | bytes 8388608
  150.7 35.6 %slice-start.5 = ((s8[6488064]{0:T(1024)(128)(4,1)}), s8[2293760]{0:T(1024)(128)(4,1)S(1)}, s32[]{:S(2)}) async-start(s8[6488064]{0:T(1024)(128)(4,1)} %bitcast.5), calls=%async_computation.5 | async-start | bytes 4587520
  150.7 35.6 %copy-start.2 = (bf16[352,3072]{1,0:T(8,128)(2,1)S(1)}, bf16[352,3072]{1,0:T(8,128)(2,1)}, u32[]{:S(2)}) copy-start(bf16[352,3072]{1,0:T(8,128)(2,1)} %refs_4_.9) | copy-start | bytes 6488068
  150.7 51.1 %collective-permute-start.5 = (bf16[176,3072]{1,0:T(8,128)(2,1)S(1)}, bf16[176,3072]{1,0:T(8,128)(2,1)S(1)}, u32[]{:S(2)}, u32[]{:S(2)}) collective-permute-start(bf16[176,3072]{1,0:T(8,128)(2,1)S(1)} %get-tuple-element.22), channel_id=1, source_target_pairs={{0,1},{1,2},{2,3},{3,0},{4,5},{5,6},{6,7},{7,4},{8,9},{9,10},{10,1... | collective-permute-start | bytes 3244040 | tf_op jit(solution)/shard_map/ppermute | solution.py:243
  152.2 3.6 %copy-start.3 = (bf16[2304,1408]{1,0:T(8,128)(2,1)S(1)}, bf16[2304,1408]{1,0:T(8,128)(2,1)}, u32[]{:S(2)}) copy-start(bf16[2304,1408]{1,0:T(8,128)(2,1)} %shard_map.83.refs_0_) | copy-start | bytes 19464196
  155.8 27.1 %copy-start.16 = (bf16[176,1536]{1,0:T(8,128)(2,1)S(1)}, bf16[176,1536]{1,0:T(8,128)(2,1)}, u32[]{:S(2)}) copy-start(bf16[176,1536]{1,0:T(8,128)(2,1)} %get-tuple-element.28) | copy-start | bytes 1622020
  155.8 27.2 %copy-start.17 = (bf16[176,1536]{1,0:T(8,128)(2,1)S(1)}, bf16[176,1536]{1,0:T(8,128)(2,1)}, u32[]{:S(2)}) copy-start(bf16[176,1536]{1,0:T(8,128)(2,1)} %get-tuple-element.26) | copy-start | bytes 1622020
  182.8 39.5 %collective-permute-start.16 = (bf16[176,1536]{1,0:T(8,128)(2,1)S(1)}, bf16[176,1536]{1,0:T(8,128)(2,1)S(1)}, u32[]{:S(2)}, u32[]{:S(2)}) collective-permute-start(bf16[176,1536]{1,0:T(8,128)(2,1)S(1)} %copy-done.16), channel_id=1, source_target_pairs={{0,1},{1,2},{2,3},{3,0},{4,5},{5,6},{6,7},{7,4},{8,9},{9,10},{10,1... | collective-permute-start | bytes 1622024 | tf_op jit(solution)/shard_map/ppermute | solution.py:243
  183.0 42.7 %collective-permute-start.17 = (bf16[176,1536]{1,0:T(8,128)(2,1)S(1)}, bf16[176,1536]{1,0:T(8,128)(2,1)S(1)}, u32[]{:S(2)}, u32[]{:S(2)}) collective-permute-start(bf16[176,1536]{1,0:T(8,128)(2,1)S(1)} %copy-done.17), channel_id=1, source_target_pairs={{0,3},{1,0},{2,1},{3,2},{4,7},{5,4},{6,5},{7,6},{8,11},{9,8},{10,9... | collective-permute-start | bytes 1622024 | tf_op jit(solution)/shard_map/ppermute | solution.py:244
  186.2 32.3 %collective-permute-start.8 = (bf16[176,3072]{1,0:T(8,128)(2,1)S(1)}, bf16[176,3072]{1,0:T(8,128)(2,1)S(1)}, u32[]{:S(2)}, u32[]{:S(2)}) collective-permute-start(bf16[176,3072]{1,0:T(8,128)(2,1)S(1)} %get-tuple-element.21), channel_id=1, source_target_pairs={{0,3},{1,0},{2,1},{3,2},{4,7},{5,4},{6,5},{7,6},{8,11},{9,8},{10,9... | collective-permute-start | bytes 3244040 | tf_op jit(solution)/shard_map/ppermute | solution.py:244
  186.3 15.5 %copy-start.9 = (f32[176,3072]{1,0:T(8,128)S(1)}, f32[176,3072]{1,0:T(8,128)}, u32[]{:S(2)}) copy-start(f32[176,3072]{1,0:T(8,128)} %copy-done.8) | copy-start | bytes 6488068
  186.3 32.2 %copy-start.7 = (f32[176,3072]{1,0:T(8,128)S(1)}, f32[176,3072]{1,0:T(8,128)}, u32[]{:S(2)}) copy-start(f32[176,3072]{1,0:T(8,128)} %copy-done.6) | copy-start | bytes 6488068
  201.8 42.8 %collective-permute-start.6 = (bf16[24,3072]{1,0:T(8,128)(2,1)S(1)}, bf16[24,3072]{1,0:T(8,128)(2,1)S(1)}, u32[]{:S(2)}, u32[]{:S(2)}) collective-permute-start(bf16[24,3072]{1,0:T(8,128)(2,1)S(1)} %add_convert_fusion.5), channel_id=1, source_target_pairs={{0,1},{1,2},{2,3},{3,0},{4,5},{5,6},{6,7},{7,4},{8,9},{9,10},{10,1... | collective-permute-start | bytes 442376 | tf_op jit(solution)/shard_map/ppermute | solution.py:243
  218.5 26.1 %collective-permute-start.9 = (bf16[24,3072]{1,0:T(8,128)(2,1)S(1)}, bf16[24,3072]{1,0:T(8,128)(2,1)S(1)}, u32[]{:S(2)}, u32[]{:S(2)}) collective-permute-start(bf16[24,3072]{1,0:T(8,128)(2,1)S(1)} %add_convert_fusion.4), channel_id=1, source_target_pairs={{0,3},{1,0},{2,1},{3,2},{4,7},{5,4},{6,5},{7,6},{8,11},{9,8},{10,9... | collective-permute-start | bytes 442376 | tf_op jit(solution)/shard_map/ppermute | solution.py:244
  222.0 19.5 %collective-permute-start.10 = (bf16[152,3072]{1,0:T(8,128)(2,1)S(1)}, bf16[152,3072]{1,0:T(8,128)(2,1)S(1)}, u32[]{:S(2)}, u32[]{:S(2)}) collective-permute-start(bf16[152,3072]{1,0:T(8,128)(2,1)S(1)} %add_convert_fusion.3), channel_id=1, source_target_pairs={{0,1},{1,2},{2,3},{3,0},{4,5},{5,6},{6,7},{7,4},{8,9},{9,10},{10,1... | collective-permute-start | bytes 2801672 | tf_op jit(solution)/shard_map/ppermute | solution.py:243
  222.1 20.6 %slice-start.6 = ((s8[4325376]{0:T(1024)(128)(4,1)}), s8[4194304]{0:T(1024)(128)(4,1)S(1)}, s32[]{:S(2)}) async-start(s8[4325376]{0:T(1024)(128)(4,1)} %bitcast.7), calls=%async_computation.6 | async-start | bytes 8388608
  222.3 20.4 %slice-start.7 = ((s8[4325376]{0:T(1024)(128)(4,1)}), s8[131072]{0:T(1024)(128)(4,1)S(1)}, s32[]{:S(2)}) async-start(s8[4325376]{0:T(1024)(128)(4,1)} %bitcast.7), calls=%async_computation.7 | async-start | bytes 262144
  222.3 20.3 %collective-permute-start.11 = (bf16[152,3072]{1,0:T(8,128)(2,1)S(1)}, bf16[152,3072]{1,0:T(8,128)(2,1)S(1)}, u32[]{:S(2)}, u32[]{:S(2)}) collective-permute-start(bf16[152,3072]{1,0:T(8,128)(2,1)S(1)} %add_convert_fusion.2), channel_id=1, source_target_pairs={{0,3},{1,0},{2,1},{3,2},{4,7},{5,4},{6,5},{7,6},{8,11},{9,8},{10,9... | collective-permute-start | bytes 2801672 | tf_op jit(solution)/shard_map/ppermute | solution.py:244
